TPU v7x, 32 devices: a whole 2x2x4 slice. The times are simulated.
32 devices in a mesh: rows: 8 (over y, x, core), model: 4 (over z).
Axes of the slice: x: 2, y: 2, z: 4, core: 2. Of those that a mesh axis runs over, the one named last changes fastest.
Arguments:
- one_query: float32 [5120, 5120], P('rows', 'model'), may hold values from -0.125 to 0.125
- other_query: float32 [5120, 5120], P('rows', 'model'), may hold values from -0.078125 to 0.078125
- one_key: float32 [5120, 5120], P('rows', 'model'), may hold values from -0.125 to 0.125
- other_key: float32 [5120, 5120], P('rows', 'model'), may hold values from -0.078125 to 0.078125
- one_value: float32 [5120, 5120], P('rows', 'model'), may hold values from -0.125 to 0.125
- other_value: float32 [5120, 5120], P('rows', 'model'), may hold values from -0.078125 to 0.078125
- mix_share: float32 [5120], P('rows'), may hold values from 0.2 to 0.8
- norm_gain: float32 [5120], P('rows'), may hold values from 0.25 to 1.75
Outputs:
- final_query: bfloat16 [5120, 5120], P(None, 'model')
- final_key: bfloat16 [5120, 5120], P(None, 'model')
- final_value: bfloat16 [5120, 5120], P(None, 'model')
- factor_query: float32 [5120], P('model')
- factor_key: float32 [5120], P('model')
- factor_value: float32 [5120], P('model')
All inputs are finite; a program needn't handle non-finite values. Where the computation divides by a largest or mean magnitude, that divisor is 1e-20 or more.
Results may differ from a plain program's by a relative error of at most 0.001.
Values may be sent and summed in bfloat16 or wider, within the bound.
No kernel may reach another device: no remote copies, remote signals or barrier semaphores. Data moves between devices by JAX's collectives and lax.ppermute only.
A program may use at most 192 MiB of HBM per device.

v0:
```python
import jax
import jax.numpy as jnp
from jax import lax
from jax.sharding import PartitionSpec as P


def local(one_query, other_query, one_key, other_key, one_value, other_value, mix_share, norm_gain):
    result_query = mix_share[:, None] * one_query + (1.0 - mix_share[:, None]) * other_query
    result_key = mix_share[:, None] * one_key + (1.0 - mix_share[:, None]) * other_key
    result_value = mix_share[:, None] * one_value + (1.0 - mix_share[:, None]) * other_value
    result_gained_query = result_query * norm_gain[:, None]
    result_gained_key = result_key * norm_gain[:, None]
    result_gained_value = result_value * norm_gain[:, None]
    factor_query, factor_key, factor_value = lax.pmax(
        (
            jnp.max(jnp.abs(result_gained_query), axis=0),
            jnp.max(jnp.abs(result_gained_key), axis=0),
            jnp.max(jnp.abs(result_gained_value), axis=0),
        ),
        "rows",
    )
    narrow_query, narrow_key, narrow_value = (
        (result_gained_query / factor_query).astype(jnp.bfloat16),
        (result_gained_key / factor_key).astype(jnp.bfloat16),
        (result_gained_value / factor_value).astype(jnp.bfloat16),
    )
    final_query, final_key, final_value = (
        lax.all_gather(narrow_query, "rows", axis=0, tiled=True),
        lax.all_gather(narrow_key, "rows", axis=0, tiled=True),
        lax.all_gather(narrow_value, "rows", axis=0, tiled=True),
    )
    return (final_query, final_key, final_value, factor_query, factor_key, factor_value)


def solution(mesh):
    placed = (
        P("rows", "model"),
        P("rows", "model"),
        P("rows", "model"),
        P("rows", "model"),
        P("rows", "model"),
        P("rows", "model"),
        P("rows"),
        P("rows"),
    )
    return jax.shard_map(
        local,
        mesh=mesh,
        in_specs=placed,
        out_specs=(
            P(None, "model"),
            P(None, "model"),
            P(None, "model"),
            P("model"),
            P("model"),
            P("model"),
        ),
        check_vma=False,
    )
```

profile of v0, /device:TPU:0, one launch (start us, length us, event | category | flops | bytes accessed | tf_op | source)
XLA Modules:
  0.0 307.9 jit_solution(9677748972599385960)
XLA Ops:
  7.2 0.0 all-gather.4.cloned.1.call-start
  7.2 0.7 broadcast_subtract_fusion
  7.9 10.6 %abs_reduce_fusion = (f32[1280]{0:T(1024)S(1)}, f32[640,1280]{1,0:T(8,128)S(1)}, f32[1280]{0:T(1024)S(1)}, f32[640,1280]{1,0:T(8,128)}, f32[1280]{0:T(1024)S(1)}, /*index=5*/f32[640,1280]{1,0:T(8,128)}) fusion(f32[640]{0:T(1024)} %param.15, f32[640,1280]{1,0:T(8,128)} %param.13, f32[640]{0:T(1024)S(1)} %broadcast_subtract_fusion, f32[640,1280]{1,0:T(8,128)} %param.12, ...), kind=kLoop, calls=%fused_computation.1 | loop fusion | flops 14741760 | bytes 29514240 | tf_op jit(solution)/shard_map/reduce_max | solution.py:18
  18.5 25.5 %all-reduce = (f32[1280]{0:T(1024)S(1)}, f32[1280]{0:T(1024)S(1)}, f32[1280]{0:T(1024)S(1)}) all-reduce(f32[1280]{0:T(1024)S(1)} %get-tuple-element.17, f32[1280]{0:T(1024)S(1)} %get-tuple-element.15, f32[1280]{0:T(1024)S(1)} %get-tuple-element.9), channel_id=1, replica_groups=mesh['rows'=8,'model'=4] {'rows'}, use_global_device_ids=true, to_apply=%region_1.0 | all-reduce | flops 3840 | bytes 30720 | tf_op jit(solution)/shard_map/pmax | solution.py:14
  44.0 0.0 copy-start.1
  44.0 0.0 copy-start.2
  44.0 0.0 copy-start.3
  44.0 3.3 %divide_convert_fusion.2 = bf16[640,1280]{1,0:T(8,128)(2,1)} fusion(f32[640,1280]{1,0:T(8,128)} %get-tuple-element.18, f32[1280]{0:T(1024)S(1)} %get-tuple-element.28), kind=kLoop, calls=%fused_computation.6 | loop fusion | flops 1638400 | bytes 4920320 | tf_op jit(solution)/shard_map/convert_element_type | solution.py:23
  47.4 0.0 all-gather.4.cloned.1.call-update
  47.4 0.0 copy-done.1
  47.4 0.0 all-gather.6.cloned.1.call-start
  47.5 0.0 copy-done.2
  47.5 3.3 %divide_convert_fusion.1 = bf16[640,1280]{1,0:T(8,128)(2,1)} fusion(f32[640,1280]{1,0:T(8,128)} %get-tuple-element.16, f32[1280]{0:T(1024)S(1)} %get-tuple-element.29), kind=kLoop, calls=%fused_computation.3 | loop fusion | flops 1638400 | bytes 4920320 | tf_op jit(solution)/shard_map/convert_element_type | solution.py:24
  50.8 0.0 all-gather.6.cloned.1.call-update
  50.8 0.0 all-gather.8.cloned.1.call-start
  50.9 0.0 copy-done.3
  50.9 1.4 divide_convert_fusion
  52.3 0.0 all-gather.8.cloned.1.call-update
  52.3 68.8 %all-gather.4.cloned.1.call-done = bf16[5120,1280]{1,0:T(8,128)(2,1)} async-done(((bf16[640,1280]{1,0:T(8,128)(2,1)}), bf16[5120,1280]{1,0:T(8,128)(2,1)}) %all-gather.4.cloned.1.call-update) | async-done | bytes 13107216 | tf_op jit(solution)/shard_map/all_gather | solution.py:28
  121.1 76.7 %all-gather.6.cloned.1.call-done = bf16[5120,1280]{1,0:T(8,128)(2,1)} async-done(((bf16[640,1280]{1,0:T(8,128)(2,1)}), bf16[5120,1280]{1,0:T(8,128)(2,1)}) %all-gather.6.cloned.1.call-update) | async-done | bytes 13107216 | tf_op jit(solution)/shard_map/all_gather | solution.py:29
  197.8 76.7 %all-gather.8.cloned.1.call-done = bf16[5120,1280]{1,0:T(8,128)(2,1)} async-done(((bf16[640,1280]{1,0:T(8,128)(2,1)}), bf16[5120,1280]{1,0:T(8,128)(2,1)}) %all-gather.8.cloned.1.call-update) | async-done | bytes 13107216 | tf_op jit(solution)/shard_map/all_gather | solution.py:30
  274.6 0.0 copy-start
  274.6 0.0 slice-start
  274.6 0.0 slice-start.1
  274.6 0.0 slice-start.2
  274.6 12.6 %copy.17 = bf16[5120,1280]{1,0:T(8,128)(2,1)} copy(bf16[5120,1280]{1,0:T(8,128)(2,1)} %all-gather.4.cloned.1.call-done) | data formatting | bytes 26214400
  287.2 0.1 copy-done
  287.3 0.0 slice-start.3
  287.3 6.6 %copy.18 = bf16[5120,1280]{1,0:T(8,128)(2,1)} copy(bf16[5120,1280]{1,0:T(8,128)(2,1)S(1)} %copy-done) | data formatting | bytes 26214400
  294.0 0.0 slice-done
  294.0 1.1 slice-done.1
  295.1 1.2 slice-done.2
  296.3 0.1 slice-done.3
  296.4 4.9 %copy.19 = bf16[5120,1280]{1,0:T(8,128)(2,1)} copy(bf16[5120,1280]{1,0:T(8,128)(2,1)S(1)} %bitcast.1) | data formatting | bytes 26214400
  (1 shorter events, 0.0 us)
Async XLA Ops:
  7.2 114.0 %all-gather.4.cloned.1.call-start = ((), (), s32[]{:S(2)}) async-start(), calls=%async_computation | async-start | bytes 14745600 | tf_op jit(solution)/shard_map/all_gather | solution.py:28
  44.0 3.4 %copy-start.1 = (f32[1280]{0:T(1024)}, f32[1280]{0:T(1024)S(1)}, u32[]{:S(2)}) copy-start(f32[1280]{0:T(1024)S(1)} %get-tuple-element.28) | copy-start | bytes 15364
  44.0 3.4 %copy-start.2 = (f32[1280]{0:T(1024)}, f32[1280]{0:T(1024)S(1)}, u32[]{:S(2)}) copy-start(f32[1280]{0:T(1024)S(1)} %get-tuple-element.29) | copy-start | bytes 15364
  44.0 6.8 %copy-start.3 = (f32[1280]{0:T(1024)}, f32[1280]{0:T(1024)S(1)}, u32[]{:S(2)}) copy-start(f32[1280]{0:T(1024)S(1)} %get-tuple-element.30) | copy-start | bytes 15364
  47.4 150.4 %all-gather.6.cloned.1.call-start = ((), (), s32[]{:S(2)}) async-start(), calls=%async_computation.1 | async-start | bytes 14745600 | tf_op jit(solution)/shard_map/all_gather | solution.py:29
  50.8 223.7 %all-gather.8.cloned.1.call-start = ((), (), s32[]{:S(2)}) async-start(), calls=%async_computation.2 | async-start | bytes 14745600 | tf_op jit(solution)/shard_map/all_gather | solution.py:30
  274.6 12.8 %copy-start = (bf16[5120,1280]{1,0:T(8,128)(2,1)S(1)}, bf16[5120,1280]{1,0:T(8,128)(2,1)}, u32[]{:S(2)}) copy-start(bf16[5120,1280]{1,0:T(8,128)(2,1)} %all-gather.6.cloned.1.call-done) | copy-start | bytes 39321604
  274.6 19.4 %slice-start = ((s8[13107200]{0:T(1024)(128)(4,1)}), s8[4194304]{0:T(1024)(128)(4,1)S(1)}, s32[]{:S(2)}) async-start(s8[13107200]{0:T(1024)(128)(4,1)} %bitcast), calls=%async_computation.3 | async-start | bytes 8388608
  274.6 20.5 %slice-start.1 = ((s8[13107200]{0:T(1024)(128)(4,1)}), s8[4194304]{0:T(1024)(128)(4,1)S(1)}, s32[]{:S(2)}) async-start(s8[13107200]{0:T(1024)(128)(4,1)} %bitcast), calls=%async_computation.4 | async-start | bytes 8388608
  274.6 21.7 %slice-start.2 = ((s8[13107200]{0:T(1024)(128)(4,1)}), s8[4194304]{0:T(1024)(128)(4,1)S(1)}, s32[]{:S(2)}) async-start(s8[13107200]{0:T(1024)(128)(4,1)} %bitcast), calls=%async_computation.5 | async-start | bytes 8388608
  287.3 9.0 %slice-start.3 = ((s8[13107200]{0:T(1024)(128)(4,1)}), s8[524288]{0:T(1024)(128)(4,1)S(1)}, s32[]{:S(2)}) async-start(s8[13107200]{0:T(1024)(128)(4,1)} %bitcast), calls=%async_computation.6 | async-start | bytes 1048576
Sparse Core Ops, SparseCore 0:
  47.5 73.5 all-gather.3
  123.6 74.1 all-gather.5
  200.3 74.1 all-gather.7
where the time goes:
time: 308 us
  waiting for transfers between devices  222 us (72%)
  local copies, waits for them, and re-layouts  26.8 us (9%)
  blocking collectives  25.5 us (8%)
  other arithmetic  19.4 us (6%)
  between operations  13.8 us (4%)
    all_gather x1, waiting for transfers between devices, local(): lax.all_gather(narrow_value, 'rows', axis=0, tiled=True)  76.7 us
    all_gather x1, waiting for transfers between devices, local(): lax.all_gather(narrow_key, 'rows', axis=0, tiled=True)  76.7 us
    all_gather x1, waiting for transfers between devices, local(): lax.all_gather(narrow_query, 'rows', axis=0, tiled=True)  68.8 us
    unnamed x19, local copies, waits for them, and re-layouts  26.8 us
    pmax x1, blocking collectives, local(): lax.pmax((jnp.max(jnp.abs(result_gained_query), axis=0), jnp.max(jnp.abs(...  25.5 us
    reduce_max x1, other arithmetic, local(): jnp.max(jnp.abs(result_gained_value), axis=0)  10.6 us
  transfers between devices with their start and end apart: 3, of which 3 were waited for; matrix products, arithmetic and copies ran while one was open for 2% of the time, Pallas kernels for 0%

commit v1 on v0

v1 whole, which is shorter than its diff:
```python
import functools

import jax
import jax.numpy as jnp
from jax import lax
from jax.experimental import pallas as pl
from jax.experimental.pallas import tpu as pltpu
from jax.sharding import PartitionSpec as P


def place_body(count, rows, *refs):
    starts, pieces = refs[0], refs[1 : 1 + count]
    out, *slots, into, back = refs[-(count + 3) :]
    ins = [pltpu.make_async_copy(pieces[k], slots[k], into.at[k]) for k in range(count)]
    outs = []
    for k in range(count):
        at = pl.multiple_of(starts[k] * 16, 16)
        outs.append(pltpu.make_async_copy(slots[k], out.at[pl.ds(at, rows[k])], back.at[k]))
        ins[k].start()
    for k in range(count):
        ins[k].wait()
        outs[k].start()
    for k in range(count):
        outs[k].wait()


def place(pieces, starts, shape, filled=None):
    count = len(pieces)
    anywhere = pl.BlockSpec(memory_space=pltpu.HBM)
    operands = [jnp.stack(starts).astype(jnp.int32) // 16, *pieces]
    aliases = {}
    if filled is not None:
        aliases = {len(operands): 0}
        operands.append(filled)
    moved = 2 * 2 * sum(p.size for p in pieces)
    return pl.pallas_call(
        functools.partial(place_body, count, [p.shape[0] for p in pieces]),
        out_shape=jax.ShapeDtypeStruct(shape, jnp.bfloat16),
        in_specs=[pl.BlockSpec(memory_space=pltpu.SMEM)] + [anywhere] * (len(operands) - 1),
        out_specs=anywhere,
        scratch_shapes=[pltpu.VMEM(p.shape, jnp.bfloat16) for p in pieces]
        + [pltpu.SemaphoreType.DMA((count,)), pltpu.SemaphoreType.DMA((count,))],
        input_output_aliases=aliases,
        cost_estimate=pl.CostEstimate(flops=0, bytes_accessed=moved, transcendentals=0),
    )(*operands)


def grid_of(n):
    pair = 2 if n % 2 == 0 else 1
    rest = n // pair
    inner = 2 if rest % 2 == 0 else 1
    return rest // inner, inner, pair


def shift(x, n, axis, by):
    dims = grid_of(n)
    table = []
    for i in range(n):
        o, rest = divmod(i, dims[1] * dims[2])
        at = [o, *divmod(rest, dims[2])]
        at[axis] = (at[axis] + by) % dims[axis]
        table.append((i, (at[0] * dims[1] + at[1]) * dims[2] + at[2]))
    return lax.ppermute(x, "rows", table)


def gather_all(halves, n, me):
    outer, inner, pair = grid_of(n)
    size = halves[0].shape[0]
    mine = (me // (inner * pair), (me // pair) % inner, me % pair)
    dims = (outer, inner, pair)

    def row(offsets, half):
        at = [(mine[a] - offsets[a]) % dims[a] for a in range(3)]
        return ((at[0] * inner + at[1]) * pair + at[2]) * (2 * size) + half * size

    early, late = [], []
    for half in (0, 1):
        early.append((halves[half], (0, 0, 0), half))
    got = {}
    for by in range(1, inner):
        for half in (0, 1):
            got[(0, by, half)] = shift(halves[half], n, 1, by)
    for by in range(1, outer):
        for half in (1, 0):
            got[(by, 0, half)] = shift(halves[half], n, 0, by)
    for (o, i, half), piece in got.items():
        early.append((piece, (o, i, 0), half))
    for o in range(1, outer):
        for i in range(1, inner):
            late.append((shift(got[(0, i, 0)], n, 0, o), (o, i, 0), 0))
            late.append((shift(got[(o, 0, 1)], n, 1, i), (o, i, 0), 1))

    def both(pieces):
        every = list(pieces)
        for by in range(1, pair):
            for piece, (o, i, _), half in pieces:
                every.append((shift(piece, n, 2, by), (o, i, by), half))
        return [p for p, _, _ in every], [row(at, half) for _, at, half in every]

    return both(early), both(late)


def gains(one, other, mix_share, norm_gain):
    return (mix_share[:, None] * one + (1.0 - mix_share[:, None]) * other) * norm_gain[:, None]


def factors_of(gained):
    tops = jnp.stack([jnp.max(jnp.abs(g), axis=0) for g in gained])
    return jnp.max(lax.all_gather(tops, "rows", axis=0), axis=0)


def halves_of(gained, factor):
    half = gained.shape[0] // 2
    return [(gained[h * half : (h + 1) * half] / factor).astype(jnp.bfloat16) for h in (0, 1)]


def local(n, *args):
    ones, others, mix_share, norm_gain = list(args[0:6:2]), list(args[1:6:2]), args[6], args[7]
    me = lax.axis_index("rows")
    first = gains(ones[0], others[0], mix_share, norm_gain)
    factors = [factors_of([first])[0]]
    halves = [halves_of(first, factors[0])]
    (ones[1:], others[1:], halves[0]) = lax.optimization_barrier((ones[1:], others[1:], halves[0]))
    rest = [gains(ones[k], others[k], mix_share, norm_gain) for k in (1, 2)]
    tops = factors_of(rest)
    factors += [tops[0], tops[1]]
    halves += [halves_of(rest[k - 1], factors[k]) for k in (1, 2)]
    plans = [gather_all(halves[k], n, me) for k in range(3)]
    finals = []
    for early, late in plans:
        shape = (first.shape[0] * n, first.shape[1])
        out = place(*early, shape)
        if late[0]:
            out = place(*late, shape, out)
        finals.append(out)
    return (*finals, *factors)


def solution(mesh):
    whole = P("rows", "model")
    return jax.shard_map(
        functools.partial(local, mesh.shape["rows"]),
        mesh=mesh,
        in_specs=(whole,) * 6 + (P("rows"),) * 2,
        out_specs=(P(None, "model"),) * 3 + (P("model"),) * 3,
        check_vma=False,
    )
```

time: 308 us -> 247 us (0.80)
  waiting for transfers between devices: 222 us -> 153 us
  Pallas kernels: 0 us -> 35.5 us
  local copies, waits for them, and re-layouts: 26.8 us -> 1.85 us
  starting transfers between devices: 0.12 us -> 20.6 us
  between operations: 13.8 us -> 1.18 us
  blocking collectives: 25.5 us -> 19.9 us
  other arithmetic: 19.4 us -> 15.2 us
    all_gather x3 -> x0, waiting for transfers between devices: 222 us -> none  [the longest x1 76.7 us: local(): lax.all_gather(narrow_value, 'rows', axis=0, tiled=True)]
    ppermute x0 -> x42, waiting for transfers between devices: none -> 153 us  [shift(): return lax.ppermute(x, 'rows', table)]
    pallas_call x0 -> x6, Pallas kernels: none -> 35.5 us  [place(): pl.pallas_call(functools.partial(place_body, count, [p.shape[0] for p in...]
    pmax x1 -> x0, blocking collectives: 25.5 us -> none  [local(): lax.pmax((jnp.max(jnp.abs(result_gained_query), axis=0), jnp.max(jnp.abs(...]
    unnamed x19 -> x89, local copies, waits for them, and re-layouts: 26.8 us -> 1.72 us
    ppermute x0 -> x42, starting transfers between devices: none -> 20.6 us  [shift(): return lax.ppermute(x, 'rows', table)]
    all_gather x0 -> x2, blocking collectives: none -> 19.9 us  [factors_of(): return jnp.max(lax.all_gather(tops, 'rows', axis=0), axis=0)]
    convert_element_type x3, other arithmetic: 8.07 us -> 3.83 us  [halves_of(): (gained[h * half:(h + 1) * half] / factor).astype(jnp.bfloat16)]
  transfers between devices with their start and end apart: 3 -> 42, of which waited for: 3 -> 18; matrix products, arithmetic and copies ran while one was open for 2% -> 1% of each run, Pallas kernels for 0% -> 13%
where the time goes in v1:
time: 247 us
  waiting for transfers between devices  153 us (62%)
  Pallas kernels  35.5 us (14%)
  starting transfers between devices  20.6 us (8%)
  blocking collectives  19.9 us (8%)
  other arithmetic  15.2 us (6%)
    ppermute x42, waiting for transfers between devices, shift(): return lax.ppermute(x, 'rows', table)  153 us
    pallas_call x6, Pallas kernels, place(): pl.pallas_call(functools.partial(place_body, count, [p.shape[0] for p in...  35.5 us
    ppermute x42, starting transfers between devices, shift(): return lax.ppermute(x, 'rows', table)  20.6 us
    all_gather x2, blocking collectives, factors_of(): return jnp.max(lax.all_gather(tops, 'rows', axis=0), axis=0)  19.9 us
    reduce_max x2, other arithmetic, factors_of(): tops = jnp.stack([jnp.max(jnp.abs(g), axis=0) for g in gained])  9.29 us
  transfers between devices with their start and end apart: 42, of which 18 were waited for; matrix products, arithmetic and copies ran while one was open for 1% of the time, Pallas kernels for 13%

profile of v1, /device:TPU:0, one launch (start us, length us, event | category | flops | bytes accessed | tf_op | source)
XLA Modules:
  0.0 246.8 jit_solution(5230706590052436382)
XLA Ops:
  0.6 0.7 broadcast_subtract_fusion
  1.3 3.6 %abs_reduce_fusion.2 = (f32[1280]{0:T(1024)S(1)}, f32[640,1280]{1,0:T(8,128)S(1)}) fusion(f32[640]{0:T(1024)} %param.15, f32[640,1280]{1,0:T(8,128)} %param.9, f32[640]{0:T(1024)S(1)} %broadcast_subtract_fusion, f32[640,1280]{1,0:T(8,128)} %param.8, f32[640]{0:T(1024)} %param.14), kind=kLoop, calls=%fused_computation.4 | loop fusion | flops 4913920 | bytes 9843200 | tf_op jit(solution)/shard_map/reduce_max | solution.py:108
  4.9 10.6 %all-gather.2 = f32[8,1,1280]{2,1,0:T(1,128)S(1)} all-gather(f32[1,1,1280]{2,1,0:T(1,128)S(1)} %reshape.22), channel_id=2, replica_groups=mesh['rows'=8,'model'=4] {'rows'}, dimensions={0}, use_global_device_ids=true | all-gather | bytes 46080 | tf_op jit(solution)/shard_map/all_gather | solution.py:109
  15.6 1.4 fusion.4
  17.1 1.1 copy-done
  18.1 5.7 %abs_reduce_fusion = (f32[1280]{0:T(1024)S(1)}, f32[640,1280]{1,0:T(8,128)}, f32[1280]{0:T(1024)S(1)}, f32[640,1280]{1,0:T(8,128)S(1)}) fusion(f32[640]{0:T(1024)S(1)} %copy-done.43, f32[640,1280]{1,0:T(8,128)S(1)} %copy-done, f32[640]{0:T(1024)S(1)} %broadcast_subtract_fusion, f32[640,1280]{1,0:T(8,128)} %param.12, f32[640]{0:T(1024)S(1)} %copy-done.39, ...), kind=kLoop, calls=%fused_computation | loop fusion | flops 9827840 | bytes 19678720 | tf_op jit(solution)/shard_map/reduce_max | solution.py:108
  23.9 9.3 %all-gather.3 = f32[8,2,1280]{2,1,0:T(2,128)S(1)} all-gather(f32[1,2,1280]{2,1,0:T(2,128)S(1)} %maximum_bitcast_fusion), channel_id=3, replica_groups=mesh['rows'=8,'model'=4] {'rows'}, dimensions={0}, use_global_device_ids=true | all-gather | bytes 92160 | tf_op jit(solution)/shard_map/all_gather | solution.py:109
  33.3 2.2 fusion
  35.5 0.6 collective-permute-start.28
  36.1 1.5 collective-permute-start.30
  37.6 0.5 collective-permute-start.34
  38.1 1.5 collective-permute-start.35
  39.9 16.8 %collective-permute-done.28.refs_3_ = bf16[320,1280]{1,0:T(8,128)(2,1)S(1)} collective-permute-done((bf16[320,1280]{1,0:T(8,128)(2,1)S(1)}, bf16[320,1280]{1,0:T(8,128)(2,1)S(1)}, u32[]{:S(2)}, u32[]{:S(2)}) %collective-permute-start.28) | collective-permute-done | bytes 819232 | tf_op jit(solution)/shard_map/ppermute | solution.py:63
  56.7 0.5 collective-permute-done.30.refs_5_
  57.2 1.5 collective-permute-start.14
  58.7 15.5 %collective-permute-done.34.refs_4_ = bf16[320,1280]{1,0:T(8,128)(2,1)S(1)} collective-permute-done((bf16[320,1280]{1,0:T(8,128)(2,1)S(1)}, bf16[320,1280]{1,0:T(8,128)(2,1)S(1)}, u32[]{:S(2)}, u32[]{:S(2)}) %collective-permute-start.34) | collective-permute-done | bytes 819232 | tf_op jit(solution)/shard_map/ppermute | solution.py:63
  74.2 0.5 collective-permute-start.16
  74.8 1.5 collective-permute-start.20
  76.3 0.5 collective-permute-start.21
  76.8 15.0 %collective-permute-done.14.refs_3_ = bf16[320,1280]{1,0:T(8,128)(2,1)S(1)} collective-permute-done((bf16[320,1280]{1,0:T(8,128)(2,1)S(1)}, bf16[320,1280]{1,0:T(8,128)(2,1)S(1)}, u32[]{:S(2)}, u32[]{:S(2)}) %collective-permute-start.14) | collective-permute-done | bytes 819232 | tf_op jit(solution)/shard_map/ppermute | solution.py:63
  91.8 3.6 %collective-permute-done.16.refs_5_ = bf16[320,1280]{1,0:T(8,128)(2,1)S(1)} collective-permute-done((bf16[320,1280]{1,0:T(8,128)(2,1)S(1)}, bf16[320,1280]{1,0:T(8,128)(2,1)S(1)}, u32[]{:S(2)}, u32[]{:S(2)}) %collective-permute-start.16) | collective-permute-done | bytes 819232 | tf_op jit(solution)/shard_map/ppermute | solution.py:63
  95.4 0.5 collective-permute-start
  95.9 13.5 %collective-permute-done.20.refs_4_ = bf16[320,1280]{1,0:T(8,128)(2,1)S(1)} collective-permute-done((bf16[320,1280]{1,0:T(8,128)(2,1)S(1)}, bf16[320,1280]{1,0:T(8,128)(2,1)S(1)}, u32[]{:S(2)}, u32[]{:S(2)}) %collective-permute-start.20) | collective-permute-done | bytes 819232 | tf_op jit(solution)/shard_map/ppermute | solution.py:63
  109.4 0.5 collective-permute-start.2
  109.9 0.9 collective-permute-done.21.refs_6_
  110.8 0.6 collective-permute-start.6
  111.4 1.5 collective-permute-start.7
  112.9 14.0 %collective-permute-done.refs_3_ = bf16[320,1280]{1,0:T(8,128)(2,1)S(1)} collective-permute-done((bf16[320,1280]{1,0:T(8,128)(2,1)S(1)}, bf16[320,1280]{1,0:T(8,128)(2,1)S(1)}, u32[]{:S(2)}, u32[]{:S(2)}) %collective-permute-start) | collective-permute-done | bytes 819232 | tf_op jit(solution)/shard_map/ppermute | solution.py:63
  126.9 3.6 %collective-permute-done.2.refs_5_ = bf16[320,1280]{1,0:T(8,128)(2,1)S(1)} collective-permute-done((bf16[320,1280]{1,0:T(8,128)(2,1)S(1)}, bf16[320,1280]{1,0:T(8,128)(2,1)S(1)}, u32[]{:S(2)}, u32[]{:S(2)}) %collective-permute-start.2) | collective-permute-done | bytes 819232 | tf_op jit(solution)/shard_map/ppermute | solution.py:63
  130.5 13.4 %collective-permute-done.6.refs_4_ = bf16[320,1280]{1,0:T(8,128)(2,1)S(1)} collective-permute-done((bf16[320,1280]{1,0:T(8,128)(2,1)S(1)}, bf16[320,1280]{1,0:T(8,128)(2,1)S(1)}, u32[]{:S(2)}, u32[]{:S(2)}) %collective-permute-start.6) | collective-permute-done | bytes 819232 | tf_op jit(solution)/shard_map/ppermute | solution.py:63
  143.8 2.1 collective-permute-done.7.refs_6_
  146.5 0.6 collective-permute-start.29
  147.1 1.6 collective-permute-start.31
  149.6 17.2 %collective-permute-done.29.refs_1_ = bf16[320,1280]{1,0:T(8,128)(2,1)S(1)} collective-permute-done((bf16[320,1280]{1,0:T(8,128)(2,1)S(1)}, bf16[320,1280]{1,0:T(8,128)(2,1)S(1)}, u32[]{:S(2)}, u32[]{:S(2)}) %collective-permute-start.29) | collective-permute-done | bytes 819232 | tf_op jit(solution)/shard_map/ppermute | solution.py:63
  167.2 1.5 collective-permute-start.15
  168.7 0.6 collective-permute-start.17
  169.9 17.6 %collective-permute-done.15.refs_1_ = bf16[320,1280]{1,0:T(8,128)(2,1)} collective-permute-done((bf16[320,1280]{1,0:T(8,128)(2,1)S(1)}, bf16[320,1280]{1,0:T(8,128)(2,1)}, u32[]{:S(2)}, u32[]{:S(2)}) %collective-permute-start.15) | collective-permute-done | bytes 819232 | tf_op jit(solution)/shard_map/ppermute | solution.py:63
  187.9 1.5 collective-permute-start.1
  189.4 0.6 collective-permute-start.3
  190.6 17.7 %collective-permute-done.1.refs_1_ = bf16[320,1280]{1,0:T(8,128)(2,1)} collective-permute-done((bf16[320,1280]{1,0:T(8,128)(2,1)S(1)}, bf16[320,1280]{1,0:T(8,128)(2,1)}, u32[]{:S(2)}, u32[]{:S(2)}) %collective-permute-start.1) | collective-permute-done | bytes 819232 | tf_op jit(solution)/shard_map/ppermute | solution.py:63
  209.9 0.7 and_select_fusion.1.refs_0_
  210.5 0.6 and_select_fusion.refs_0_
  211.1 8.3 %shard_map.131.refs_5_ = bf16[5120,1280]{1,0:T(8,128)(2,1)} custom-call(s32[12]{0:T(128)} %and_select_fusion.refs_0_, bf16[320,1280]{1,0:T(8,128)(2,1)} %copy-done.4, bf16[320,1280]{1,0:T(8,128)(2,1)} %copy-done.3, bf16[320,1280]{1,0:T(8,128)(2,1)} %copy-done.7, bf16[320,1280]{1,0:T(8,128)(2,1)} %copy-done.9, bf16[320,1280]{1,0:T(8,128)(2,1)} %copy-done.8, ...), custom_call_target="tpu_custom_call" | custom-call | bytes 19660800 | tf_op jit(solution)/shard_map/pallas_call | solution.py:36
  219.4 8.3 %shard_map.129.refs_5_ = bf16[5120,1280]{1,0:T(8,128)(2,1)} custom-call(s32[12]{0:T(128)} %and_select_fusion.refs_0_, bf16[320,1280]{1,0:T(8,128)(2,1)} %copy-done.6, bf16[320,1280]{1,0:T(8,128)(2,1)} %copy-done.5, bf16[320,1280]{1,0:T(8,128)(2,1)} %copy-done.12, bf16[320,1280]{1,0:T(8,128)(2,1)} %copy-done.15, bf16[320,1280]{1,0:T(8,128)(2,1)} %copy-done.14, ...), custom_call_target="tpu_custom_call" | custom-call | bytes 19660800 | tf_op jit(solution)/shard_map/pallas_call | solution.py:36
  227.7 8.3 %shard_map.127.refs_5_ = bf16[5120,1280]{1,0:T(8,128)(2,1)} custom-call(s32[12]{0:T(128)} %and_select_fusion.refs_0_, bf16[320,1280]{1,0:T(8,128)(2,1)} %get-tuple-element.12.refs_1_, bf16[320,1280]{1,0:T(8,128)(2,1)} %get-tuple-element.13.refs_2_, bf16[320,1280]{1,0:T(8,128)(2,1)} %copy-done.18, bf16[320,1280]{1,0:T(8,128)(2,1)} %copy-done.21, ...), custom_call_target="tpu_custom_call" | custom-call | bytes 19660800 | tf_op jit(solution)/shard_map/pallas_call | solution.py:36
  236.0 3.6 %shard_map.132 = bf16[5120,1280]{1,0:T(8,128)(2,1)} custom-call(s32[4]{0:T(128)} %and_select_fusion.1.refs_0_, bf16[320,1280]{1,0:T(8,128)(2,1)} %copy-done.25, bf16[320,1280]{1,0:T(8,128)(2,1)} %collective-permute-done.31.refs_2_, bf16[320,1280]{1,0:T(8,128)(2,1)} %copy-done.38, ...), custom_call_target="tpu_custom_call", output_to_operand_aliasing={{}: (5, {})} | custom-call | bytes 6553600 | tf_op jit(solution)/shard_map/pallas_call | solution.py:36
  239.6 3.6 %shard_map.130 = bf16[5120,1280]{1,0:T(8,128)(2,1)} custom-call(s32[4]{0:T(128)} %and_select_fusion.1.refs_0_, bf16[320,1280]{1,0:T(8,128)(2,1)} %collective-permute-done.15.refs_1_, bf16[320,1280]{1,0:T(8,128)(2,1)} %collective-permute-done.17.refs_2_, bf16[320,1280]{1,0:T(8,128)(2,1)} %collective-permute-done.18.refs_3_, ...), custom_call_target="tpu_custom_call", output_to_operand_aliasing={{}: (5, {})} | custom-call | bytes 6553600 | tf_op jit(solution)/shard_map/pallas_call | solution.py:36
  243.2 3.6 %shard_map.128 = bf16[5120,1280]{1,0:T(8,128)(2,1)} custom-call(s32[4]{0:T(128)} %and_select_fusion.1.refs_0_, bf16[320,1280]{1,0:T(8,128)(2,1)} %collective-permute-done.1.refs_1_, bf16[320,1280]{1,0:T(8,128)(2,1)} %collective-permute-done.3.refs_2_, bf16[320,1280]{1,0:T(8,128)(2,1)} %collective-permute-done.4.refs_3_, ...), custom_call_target="tpu_custom_call", output_to_operand_aliasing={{}: (5, {})} | custom-call | bytes 6553600 | tf_op jit(solution)/shard_map/pallas_call | solution.py:36
  (148 shorter events, 5.4 us)
Async XLA Ops:
  35.5 111.0 %copy-start.3 = (bf16[320,1280]{1,0:T(8,128)(2,1)}, bf16[320,1280]{1,0:T(8,128)(2,1)S(1)}, u32[]{:S(2)}) copy-start(bf16[320,1280]{1,0:T(8,128)(2,1)S(1)} %get-tuple-element.26.refs_2_) | copy-start | bytes 2457604
  35.5 111.6 %copy-start.4 = (bf16[320,1280]{1,0:T(8,128)(2,1)}, bf16[320,1280]{1,0:T(8,128)(2,1)S(1)}, u32[]{:S(2)}) copy-start(bf16[320,1280]{1,0:T(8,128)(2,1)S(1)} %get-tuple-element.27.refs_1_) | copy-start | bytes 2457604
  35.5 21.2 %collective-permute-start.28 = (bf16[320,1280]{1,0:T(8,128)(2,1)S(1)}, bf16[320,1280]{1,0:T(8,128)(2,1)S(1)}, u32[]{:S(2)}, u32[]{:S(2)}) collective-permute-start(bf16[320,1280]{1,0:T(8,128)(2,1)S(1)} %get-tuple-element.27.refs_1_), channel_id=1, source_target_pairs={{0,8},{4,12},{8,0},{12,4},{16,24},{20,28},{24,16},{28,20},{1,9},{5... | collective-permute-start | bytes 2457608 | tf_op jit(solution)/shard_map/ppermute | solution.py:63
  36.1 21.1 %collective-permute-start.30 = (bf16[320,1280]{1,0:T(8,128)(2,1)S(1)}, bf16[320,1280]{1,0:T(8,128)(2,1)S(1)}, u32[]{:S(2)}, u32[]{:S(2)}) collective-permute-start(bf16[320,1280]{1,0:T(8,128)(2,1)S(1)} %get-tuple-element.26.refs_2_), channel_id=1, source_target_pairs={{0,16},{4,20},{8,24},{12,28},{16,0},{20,4},{24,8},{28,12},{1,17},{... | collective-permute-start | bytes 2457608 | tf_op jit(solution)/shard_map/ppermute | solution.py:63
  37.6 36.6 %collective-permute-start.34 = (bf16[320,1280]{1,0:T(8,128)(2,1)S(1)}, bf16[320,1280]{1,0:T(8,128)(2,1)S(1)}, u32[]{:S(2)}, u32[]{:S(2)}) collective-permute-start(bf16[320,1280]{1,0:T(8,128)(2,1)S(1)} %get-tuple-element.26.refs_2_), channel_id=1, source_target_pairs={{0,8},{4,12},{8,0},{12,4},{16,24},{20,28},{24,16},{28,20},{1,9},{5... | collective-permute-start | bytes 2457608 | tf_op jit(solution)/shard_map/ppermute | solution.py:63
  38.1 36.7 %collective-permute-start.35 = (bf16[320,1280]{1,0:T(8,128)(2,1)S(1)}, bf16[320,1280]{1,0:T(8,128)(2,1)S(1)}, u32[]{:S(2)}, u32[]{:S(2)}) collective-permute-start(bf16[320,1280]{1,0:T(8,128)(2,1)S(1)} %get-tuple-element.27.refs_1_), channel_id=1, source_target_pairs={{0,16},{4,20},{8,24},{12,28},{16,0},{20,4},{24,8},{28,12},{1,17},{... | collective-permute-start | bytes 2457608 | tf_op jit(solution)/shard_map/ppermute | solution.py:63
  39.6 36.7 %collective-permute-start.36 = (bf16[320,1280]{1,0:T(8,128)(2,1)S(1)}, bf16[320,1280]{1,0:T(8,128)(2,1)S(1)}, u32[]{:S(2)}, u32[]{:S(2)}) collective-permute-start(bf16[320,1280]{1,0:T(8,128)(2,1)S(1)} %get-tuple-element.27.refs_1_), channel_id=1, source_target_pairs={{0,4},{4,0},{8,12},{12,8},{16,20},{20,16},{24,28},{28,24},{1,5},{5... | collective-permute-start | bytes 2457608 | tf_op jit(solution)/shard_map/ppermute | solution.py:63
  56.7 20.1 %collective-permute-start.37 = (bf16[320,1280]{1,0:T(8,128)(2,1)S(1)}, bf16[320,1280]{1,0:T(8,128)(2,1)S(1)}, u32[]{:S(2)}, u32[]{:S(2)}) collective-permute-start(bf16[320,1280]{1,0:T(8,128)(2,1)S(1)} %get-tuple-element.26.refs_2_), channel_id=1, source_target_pairs={{0,4},{4,0},{8,12},{12,8},{16,20},{20,16},{24,28},{28,24},{1,5},{5... | collective-permute-start | bytes 2457608 | tf_op jit(solution)/shard_map/ppermute | solution.py:63
  57.2 34.6 %collective-permute-start.14 = (bf16[320,1280]{1,0:T(8,128)(2,1)S(1)}, bf16[320,1280]{1,0:T(8,128)(2,1)S(1)}, u32[]{:S(2)}, u32[]{:S(2)}) collective-permute-start(bf16[320,1280]{1,0:T(8,128)(2,1)S(1)} %get-tuple-element.29.refs_1_), channel_id=1, source_target_pairs={{0,8},{4,12},{8,0},{12,4},{16,24},{20,28},{24,16},{28,20},{1,9},{5... | collective-permute-start | bytes 2457608 | tf_op jit(solution)/shard_map/ppermute | solution.py:63
  74.2 21.1 %collective-permute-start.16 = (bf16[320,1280]{1,0:T(8,128)(2,1)S(1)}, bf16[320,1280]{1,0:T(8,128)(2,1)S(1)}, u32[]{:S(2)}, u32[]{:S(2)}) collective-permute-start(bf16[320,1280]{1,0:T(8,128)(2,1)S(1)} %get-tuple-element.28.refs_2_), channel_id=1, source_target_pairs={{0,16},{4,20},{8,24},{12,28},{16,0},{20,4},{24,8},{28,12},{1,17},{... | collective-permute-start | bytes 2457608 | tf_op jit(solution)/shard_map/ppermute | solution.py:63
  74.8 34.6 %collective-permute-start.20 = (bf16[320,1280]{1,0:T(8,128)(2,1)S(1)}, bf16[320,1280]{1,0:T(8,128)(2,1)S(1)}, u32[]{:S(2)}, u32[]{:S(2)}) collective-permute-start(bf16[320,1280]{1,0:T(8,128)(2,1)S(1)} %get-tuple-element.28.refs_2_), channel_id=1, source_target_pairs={{0,8},{4,12},{8,0},{12,4},{16,24},{20,28},{24,16},{28,20},{1,9},{5... | collective-permute-start | bytes 2457608 | tf_op jit(solution)/shard_map/ppermute | solution.py:63
  76.3 34.5 %collective-permute-start.21 = (bf16[320,1280]{1,0:T(8,128)(2,1)S(1)}, bf16[320,1280]{1,0:T(8,128)(2,1)S(1)}, u32[]{:S(2)}, u32[]{:S(2)}) collective-permute-start(bf16[320,1280]{1,0:T(8,128)(2,1)S(1)} %get-tuple-element.29.refs_1_), channel_id=1, source_target_pairs={{0,16},{4,20},{8,24},{12,28},{16,0},{20,4},{24,8},{28,12},{1,17},{... | collective-permute-start | bytes 2457608 | tf_op jit(solution)/shard_map/ppermute | solution.py:63
  76.8 134.3 %copy-start.13 = (bf16[320,1280]{1,0:T(8,128)(2,1)}, bf16[320,1280]{1,0:T(8,128)(2,1)S(1)}, u32[]{:S(2)}) copy-start(bf16[320,1280]{1,0:T(8,128)(2,1)S(1)} %collective-permute-done.37.refs_8_) | copy-start | bytes 2457604
  76.8 34.6 %collective-permute-start.22 = (bf16[320,1280]{1,0:T(8,128)(2,1)S(1)}, bf16[320,1280]{1,0:T(8,128)(2,1)S(1)}, u32[]{:S(2)}, u32[]{:S(2)}) collective-permute-start(bf16[320,1280]{1,0:T(8,128)(2,1)S(1)} %get-tuple-element.29.refs_1_), channel_id=1, source_target_pairs={{0,4},{4,0},{8,12},{12,8},{16,20},{20,16},{24,28},{28,24},{1,5},{5... | collective-permute-start | bytes 2457608 | tf_op jit(solution)/shard_map/ppermute | solution.py:63
  91.8 127.6 %copy-start.12 = (bf16[320,1280]{1,0:T(8,128)(2,1)}, bf16[320,1280]{1,0:T(8,128)(2,1)S(1)}, u32[]{:S(2)}) copy-start(bf16[320,1280]{1,0:T(8,128)(2,1)S(1)} %collective-permute-done.14.refs_3_) | copy-start | bytes 2457604
  91.8 21.1 %collective-permute-start.23 = (bf16[320,1280]{1,0:T(8,128)(2,1)S(1)}, bf16[320,1280]{1,0:T(8,128)(2,1)S(1)}, u32[]{:S(2)}, u32[]{:S(2)}) collective-permute-start(bf16[320,1280]{1,0:T(8,128)(2,1)S(1)} %get-tuple-element.28.refs_2_), channel_id=1, source_target_pairs={{0,4},{4,0},{8,12},{12,8},{16,20},{20,16},{24,28},{28,24},{1,5},{5... | collective-permute-start | bytes 2457608 | tf_op jit(solution)/shard_map/ppermute | solution.py:63
  95.4 124.1 %copy-start.14 = (bf16[320,1280]{1,0:T(8,128)(2,1)}, bf16[320,1280]{1,0:T(8,128)(2,1)S(1)}, u32[]{:S(2)}) copy-start(bf16[320,1280]{1,0:T(8,128)(2,1)S(1)} %collective-permute-done.16.refs_5_) | copy-start | bytes 2457604
  95.4 31.5 %collective-permute-start = (bf16[320,1280]{1,0:T(8,128)(2,1)S(1)}, bf16[320,1280]{1,0:T(8,128)(2,1)S(1)}, u32[]{:S(2)}, u32[]{:S(2)}) collective-permute-start(bf16[320,1280]{1,0:T(8,128)(2,1)S(1)} %copy-done.2), channel_id=1, source_target_pairs={{0,8},{4,12},{8,0},{12,4},{16,24},{20,28},{24,16},{28,20},{1,9},{5... | collective-permute-start | bytes 2457608 | tf_op jit(solution)/shard_map/ppermute | solution.py:63
  109.3 110.1 %copy-start.15 = (bf16[320,1280]{1,0:T(8,128)(2,1)}, bf16[320,1280]{1,0:T(8,128)(2,1)S(1)}, u32[]{:S(2)}) copy-start(bf16[320,1280]{1,0:T(8,128)(2,1)S(1)} %collective-permute-done.20.refs_4_) | copy-start | bytes 2457604
  109.4 21.1 %collective-permute-start.2 = (bf16[320,1280]{1,0:T(8,128)(2,1)S(1)}, bf16[320,1280]{1,0:T(8,128)(2,1)S(1)}, u32[]{:S(2)}, u32[]{:S(2)}) collective-permute-start(bf16[320,1280]{1,0:T(8,128)(2,1)S(1)} %copy-done.1), channel_id=1, source_target_pairs={{0,16},{4,20},{8,24},{12,28},{16,0},{20,4},{24,8},{28,12},{1,17},{... | collective-permute-start | bytes 2457608 | tf_op jit(solution)/shard_map/ppermute | solution.py:63
  110.8 33.0 %collective-permute-start.6 = (bf16[320,1280]{1,0:T(8,128)(2,1)S(1)}, bf16[320,1280]{1,0:T(8,128)(2,1)S(1)}, u32[]{:S(2)}, u32[]{:S(2)}) collective-permute-start(bf16[320,1280]{1,0:T(8,128)(2,1)S(1)} %copy-done.1), channel_id=1, source_target_pairs={{0,8},{4,12},{8,0},{12,4},{16,24},{20,28},{24,16},{28,20},{1,9},{5... | collective-permute-start | bytes 2457608 | tf_op jit(solution)/shard_map/ppermute | solution.py:63
  111.4 34.5 %collective-permute-start.7 = (bf16[320,1280]{1,0:T(8,128)(2,1)S(1)}, bf16[320,1280]{1,0:T(8,128)(2,1)S(1)}, u32[]{:S(2)}, u32[]{:S(2)}) collective-permute-start(bf16[320,1280]{1,0:T(8,128)(2,1)S(1)} %copy-done.2), channel_id=1, source_target_pairs={{0,16},{4,20},{8,24},{12,28},{16,0},{20,4},{24,8},{28,12},{1,17},{... | collective-permute-start | bytes 2457608 | tf_op jit(solution)/shard_map/ppermute | solution.py:63
  112.9 33.1 %collective-permute-start.8 = (bf16[320,1280]{1,0:T(8,128)(2,1)S(1)}, bf16[320,1280]{1,0:T(8,128)(2,1)S(1)}, u32[]{:S(2)}, u32[]{:S(2)}) collective-permute-start(bf16[320,1280]{1,0:T(8,128)(2,1)S(1)} %copy-done.2), channel_id=1, source_target_pairs={{0,4},{4,0},{8,12},{12,8},{16,20},{20,16},{24,28},{28,24},{1,5},{5... | collective-permute-start | bytes 2457608 | tf_op jit(solution)/shard_map/ppermute | solution.py:63
  126.9 19.5 %collective-permute-start.9 = (bf16[320,1280]{1,0:T(8,128)(2,1)S(1)}, bf16[320,1280]{1,0:T(8,128)(2,1)S(1)}, u32[]{:S(2)}, u32[]{:S(2)}) collective-permute-start(bf16[320,1280]{1,0:T(8,128)(2,1)S(1)} %copy-done.1), channel_id=1, source_target_pairs={{0,4},{4,0},{8,12},{12,8},{16,20},{20,16},{24,28},{28,24},{1,5},{5... | collective-permute-start | bytes 2457608 | tf_op jit(solution)/shard_map/ppermute | solution.py:63
  130.5 16.6 %collective-permute-start.38 = (bf16[320,1280]{1,0:T(8,128)(2,1)S(1)}, bf16[320,1280]{1,0:T(8,128)(2,1)S(1)}, u32[]{:S(2)}, u32[]{:S(2)}) collective-permute-start(bf16[320,1280]{1,0:T(8,128)(2,1)S(1)} %collective-permute-done.28.refs_3_), channel_id=1, source_target_pairs={{0,4},{4,0},{8,12},{12,8},{16,20},{20,16},{24,28},{28,24},{1,5},{5... | collective-permute-start | bytes 2457608 | tf_op jit(solution)/shard_map/ppermute | solution.py:63
  143.8 4.8 %collective-permute-start.40 = (bf16[320,1280]{1,0:T(8,128)(2,1)S(1)}, bf16[320,1280]{1,0:T(8,128)(2,1)S(1)}, u32[]{:S(2)}, u32[]{:S(2)}) collective-permute-start(bf16[320,1280]{1,0:T(8,128)(2,1)S(1)} %collective-permute-done.30.refs_5_), channel_id=1, source_target_pairs={{0,4},{4,0},{8,12},{12,8},{16,20},{20,16},{24,28},{28,24},{1,5},{5... | collective-permute-start | bytes 2457608 | tf_op jit(solution)/shard_map/ppermute | solution.py:63
  145.9 2.8 %collective-permute-start.39 = (bf16[320,1280]{1,0:T(8,128)(2,1)S(1)}, bf16[320,1280]{1,0:T(8,128)(2,1)S(1)}, u32[]{:S(2)}, u32[]{:S(2)}) collective-permute-start(bf16[320,1280]{1,0:T(8,128)(2,1)S(1)} %collective-permute-done.34.refs_4_), channel_id=1, source_target_pairs={{0,4},{4,0},{8,12},{12,8},{16,20},{20,16},{24,28},{28,24},{1,5},{5... | collective-permute-start | bytes 2457608 | tf_op jit(solution)/shard_map/ppermute | solution.py:63
  145.9 3.5 %collective-permute-start.41 = (bf16[320,1280]{1,0:T(8,128)(2,1)S(1)}, bf16[320,1280]{1,0:T(8,128)(2,1)S(1)}, u32[]{:S(2)}, u32[]{:S(2)}) collective-permute-start(bf16[320,1280]{1,0:T(8,128)(2,1)S(1)} %collective-permute-done.35.refs_6_), channel_id=1, source_target_pairs={{0,4},{4,0},{8,12},{12,8},{16,20},{20,16},{24,28},{28,24},{1,5},{5... | collective-permute-start | bytes 2457608 | tf_op jit(solution)/shard_map/ppermute | solution.py:63
  146.5 20.3 %collective-permute-start.29 = (bf16[320,1280]{1,0:T(8,128)(2,1)S(1)}, bf16[320,1280]{1,0:T(8,128)(2,1)S(1)}, u32[]{:S(2)}, u32[]{:S(2)}) collective-permute-start(bf16[320,1280]{1,0:T(8,128)(2,1)S(1)} %collective-permute-done.28.refs_3_), channel_id=1, source_target_pairs={{0,16},{4,20},{8,24},{12,28},{16,0},{20,4},{24,8},{28,12},{1,17},{... | collective-permute-start | bytes 2457608 | tf_op jit(solution)/shard_map/ppermute | solution.py:63
  147.1 20.1 %collective-permute-start.31 = (bf16[320,1280]{1,0:T(8,128)(2,1)S(1)}, bf16[320,1280]{1,0:T(8,128)(2,1)}, u32[]{:S(2)}, u32[]{:S(2)}) collective-permute-start(bf16[320,1280]{1,0:T(8,128)(2,1)S(1)} %collective-permute-done.30.refs_5_), channel_id=1, source_target_pairs={{0,8},{4,12},{8,0},{12,4},{16,24},{20,28},{24,16},{28,20},{1,9},{5... | collective-permute-start | bytes 2457608 | tf_op jit(solution)/shard_map/ppermute | solution.py:63
  148.6 20.0 %collective-permute-start.24 = (bf16[320,1280]{1,0:T(8,128)(2,1)S(1)}, bf16[320,1280]{1,0:T(8,128)(2,1)S(1)}, u32[]{:S(2)}, u32[]{:S(2)}) collective-permute-start(bf16[320,1280]{1,0:T(8,128)(2,1)S(1)} %collective-permute-done.14.refs_3_), channel_id=1, source_target_pairs={{0,4},{4,0},{8,12},{12,8},{16,20},{20,16},{24,28},{28,24},{1,5},{5... | collective-permute-start | bytes 2457608 | tf_op jit(solution)/shard_map/ppermute | solution.py:63
  148.7 20.6 %collective-permute-start.26 = (bf16[320,1280]{1,0:T(8,128)(2,1)S(1)}, bf16[320,1280]{1,0:T(8,128)(2,1)S(1)}, u32[]{:S(2)}, u32[]{:S(2)}) collective-permute-start(bf16[320,1280]{1,0:T(8,128)(2,1)S(1)} %collective-permute-done.16.refs_5_), channel_id=1, source_target_pairs={{0,4},{4,0},{8,12},{12,8},{16,20},{20,16},{24,28},{28,24},{1,5},{5... | collective-permute-start | bytes 2457608 | tf_op jit(solution)/shard_map/ppermute | solution.py:63
  149.4 19.9 %collective-permute-start.25 = (bf16[320,1280]{1,0:T(8,128)(2,1)S(1)}, bf16[320,1280]{1,0:T(8,128)(2,1)S(1)}, u32[]{:S(2)}, u32[]{:S(2)}) collective-permute-start(bf16[320,1280]{1,0:T(8,128)(2,1)S(1)} %collective-permute-done.20.refs_4_), channel_id=1, source_target_pairs={{0,4},{4,0},{8,12},{12,8},{16,20},{20,16},{24,28},{28,24},{1,5},{5... | collective-permute-start | bytes 2457608 | tf_op jit(solution)/shard_map/ppermute | solution.py:63
  166.7 3.1 %collective-permute-start.27 = (bf16[320,1280]{1,0:T(8,128)(2,1)S(1)}, bf16[320,1280]{1,0:T(8,128)(2,1)S(1)}, u32[]{:S(2)}, u32[]{:S(2)}) collective-permute-start(bf16[320,1280]{1,0:T(8,128)(2,1)S(1)} %collective-permute-done.21.refs_6_), channel_id=1, source_target_pairs={{0,4},{4,0},{8,12},{12,8},{16,20},{20,16},{24,28},{28,24},{1,5},{5... | collective-permute-start | bytes 2457608 | tf_op jit(solution)/shard_map/ppermute | solution.py:63
  167.2 20.3 %collective-permute-start.15 = (bf16[320,1280]{1,0:T(8,128)(2,1)S(1)}, bf16[320,1280]{1,0:T(8,128)(2,1)}, u32[]{:S(2)}, u32[]{:S(2)}) collective-permute-start(bf16[320,1280]{1,0:T(8,128)(2,1)S(1)} %collective-permute-done.14.refs_3_), channel_id=1, source_target_pairs={{0,16},{4,20},{8,24},{12,28},{16,0},{20,4},{24,8},{28,12},{1,17},{... | collective-permute-start | bytes 2457608 | tf_op jit(solution)/shard_map/ppermute | solution.py:63
  168.7 19.2 %collective-permute-start.17 = (bf16[320,1280]{1,0:T(8,128)(2,1)S(1)}, bf16[320,1280]{1,0:T(8,128)(2,1)}, u32[]{:S(2)}, u32[]{:S(2)}) collective-permute-start(bf16[320,1280]{1,0:T(8,128)(2,1)S(1)} %collective-permute-done.16.refs_5_), channel_id=1, source_target_pairs={{0,8},{4,12},{8,0},{12,4},{16,24},{20,28},{24,16},{28,20},{1,9},{5... | collective-permute-start | bytes 2457608 | tf_op jit(solution)/shard_map/ppermute | solution.py:63
  169.3 20.1 %collective-permute-start.10 = (bf16[320,1280]{1,0:T(8,128)(2,1)S(1)}, bf16[320,1280]{1,0:T(8,128)(2,1)S(1)}, u32[]{:S(2)}, u32[]{:S(2)}) collective-permute-start(bf16[320,1280]{1,0:T(8,128)(2,1)S(1)} %collective-permute-done.refs_3_), channel_id=1, source_target_pairs={{0,4},{4,0},{8,12},{12,8},{16,20},{20,16},{24,28},{28,24},{1,5},{5... | collective-permute-start | bytes 2457608 | tf_op jit(solution)/shard_map/ppermute | solution.py:63
  169.3 20.6 %collective-permute-start.12 = (bf16[320,1280]{1,0:T(8,128)(2,1)S(1)}, bf16[320,1280]{1,0:T(8,128)(2,1)S(1)}, u32[]{:S(2)}, u32[]{:S(2)}) collective-permute-start(bf16[320,1280]{1,0:T(8,128)(2,1)S(1)} %collective-permute-done.2.refs_5_), channel_id=1, source_target_pairs={{0,4},{4,0},{8,12},{12,8},{16,20},{20,16},{24,28},{28,24},{1,5},{5... | collective-permute-start | bytes 2457608 | tf_op jit(solution)/shard_map/ppermute | solution.py:63
  169.8 20.2 %collective-permute-start.11 = (bf16[320,1280]{1,0:T(8,128)(2,1)S(1)}, bf16[320,1280]{1,0:T(8,128)(2,1)S(1)}, u32[]{:S(2)}, u32[]{:S(2)}) collective-permute-start(bf16[320,1280]{1,0:T(8,128)(2,1)S(1)} %collective-permute-done.6.refs_4_), channel_id=1, source_target_pairs={{0,4},{4,0},{8,12},{12,8},{16,20},{20,16},{24,28},{28,24},{1,5},{5... | collective-permute-start | bytes 2457608 | tf_op jit(solution)/shard_map/ppermute | solution.py:63
  187.5 3.0 %collective-permute-start.13 = (bf16[320,1280]{1,0:T(8,128)(2,1)S(1)}, bf16[320,1280]{1,0:T(8,128)(2,1)S(1)}, u32[]{:S(2)}, u32[]{:S(2)}) collective-permute-start(bf16[320,1280]{1,0:T(8,128)(2,1)S(1)} %collective-permute-done.7.refs_6_), channel_id=1, source_target_pairs={{0,4},{4,0},{8,12},{12,8},{16,20},{20,16},{24,28},{28,24},{1,5},{5... | collective-permute-start | bytes 2457608 | tf_op jit(solution)/shard_map/ppermute | solution.py:63
  187.9 20.4 %collective-permute-start.1 = (bf16[320,1280]{1,0:T(8,128)(2,1)S(1)}, bf16[320,1280]{1,0:T(8,128)(2,1)}, u32[]{:S(2)}, u32[]{:S(2)}) collective-permute-start(bf16[320,1280]{1,0:T(8,128)(2,1)S(1)} %collective-permute-done.refs_3_), channel_id=1, source_target_pairs={{0,16},{4,20},{8,24},{12,28},{16,0},{20,4},{24,8},{28,12},{1,17},{... | collective-permute-start | bytes 2457608 | tf_op jit(solution)/shard_map/ppermute | solution.py:63
  189.4 19.3 %collective-permute-start.3 = (bf16[320,1280]{1,0:T(8,128)(2,1)S(1)}, bf16[320,1280]{1,0:T(8,128)(2,1)}, u32[]{:S(2)}, u32[]{:S(2)}) collective-permute-start(bf16[320,1280]{1,0:T(8,128)(2,1)S(1)} %collective-permute-done.2.refs_5_), channel_id=1, source_target_pairs={{0,8},{4,12},{8,0},{12,4},{16,24},{20,28},{24,16},{28,20},{1,9},{5... | collective-permute-start | bytes 2457608 | tf_op jit(solution)/shard_map/ppermute | solution.py:63
  190.0 18.9 %collective-permute-start.32 = (bf16[320,1280]{1,0:T(8,128)(2,1)S(1)}, bf16[320,1280]{1,0:T(8,128)(2,1)S(1)}, u32[]{:S(2)}, u32[]{:S(2)}) collective-permute-start(bf16[320,1280]{1,0:T(8,128)(2,1)S(1)} %collective-permute-done.29.refs_1_), channel_id=1, source_target_pairs={{0,4},{4,0},{8,12},{12,8},{16,20},{20,16},{24,28},{28,24},{1,5},{5... | collective-permute-start | bytes 2457608 | tf_op jit(solution)/shard_map/ppermute | solution.py:63
  190.0 46.0 %collective-permute-start.33 = (bf16[320,1280]{1,0:T(8,128)(2,1)}, bf16[320,1280]{1,0:T(8,128)(2,1)}, u32[]{:S(2)}, u32[]{:S(2)}) collective-permute-start(bf16[320,1280]{1,0:T(8,128)(2,1)} %collective-permute-done.31.refs_2_), channel_id=1, source_target_pairs={{0,4},{4,0},{8,12},{12,8},{16,20},{20,16},{24,28},{28,24},{1,5},{5... | collective-permute-start | bytes 2457608 | tf_op jit(solution)/shard_map/ppermute | solution.py:63
  190.5 49.1 %collective-permute-start.18 = (bf16[320,1280]{1,0:T(8,128)(2,1)}, bf16[320,1280]{1,0:T(8,128)(2,1)}, u32[]{:S(2)}, u32[]{:S(2)}) collective-permute-start(bf16[320,1280]{1,0:T(8,128)(2,1)} %collective-permute-done.15.refs_1_), channel_id=1, source_target_pairs={{0,4},{4,0},{8,12},{12,8},{16,20},{20,16},{24,28},{28,24},{1,5},{5... | collective-permute-start | bytes 2457608 | tf_op jit(solution)/shard_map/ppermute | solution.py:63
  208.3 31.3 %collective-permute-start.19 = (bf16[320,1280]{1,0:T(8,128)(2,1)}, bf16[320,1280]{1,0:T(8,128)(2,1)}, u32[]{:S(2)}, u32[]{:S(2)}) collective-permute-start(bf16[320,1280]{1,0:T(8,128)(2,1)} %collective-permute-done.17.refs_2_), channel_id=1, source_target_pairs={{0,4},{4,0},{8,12},{12,8},{16,20},{20,16},{24,28},{28,24},{1,5},{5... | collective-permute-start | bytes 2457608 | tf_op jit(solution)/shard_map/ppermute | solution.py:63
  208.6 34.5 %collective-permute-start.4 = (bf16[320,1280]{1,0:T(8,128)(2,1)}, bf16[320,1280]{1,0:T(8,128)(2,1)}, u32[]{:S(2)}, u32[]{:S(2)}) collective-permute-start(bf16[320,1280]{1,0:T(8,128)(2,1)} %collective-permute-done.1.refs_1_), channel_id=1, source_target_pairs={{0,4},{4,0},{8,12},{12,8},{16,20},{20,16},{24,28},{28,24},{1,5},{5... | collective-permute-start | bytes 2457608 | tf_op jit(solution)/shard_map/ppermute | solution.py:63
  208.9 34.3 %collective-permute-start.5 = (bf16[320,1280]{1,0:T(8,128)(2,1)}, bf16[320,1280]{1,0:T(8,128)(2,1)}, u32[]{:S(2)}, u32[]{:S(2)}) collective-permute-start(bf16[320,1280]{1,0:T(8,128)(2,1)} %collective-permute-done.3.refs_2_), channel_id=1, source_target_pairs={{0,4},{4,0},{8,12},{12,8},{16,20},{20,16},{24,28},{28,24},{1,5},{5... | collective-permute-start | bytes 2457608 | tf_op jit(solution)/shard_map/ppermute | solution.py:63
  (38 other events, 2046.9 us)

commit v2 on v1

--- a/solution.py
+++ b/solution.py
@@ -117,18 +117,14 @@
 def local(n, *args):
     ones, others, mix_share, norm_gain = list(args[0:6:2]), list(args[1:6:2]), args[6], args[7]
     me = lax.axis_index("rows")
-    first = gains(ones[0], others[0], mix_share, norm_gain)
-    factors = [factors_of([first])[0]]
-    halves = [halves_of(first, factors[0])]
-    (ones[1:], others[1:], halves[0]) = lax.optimization_barrier((ones[1:], others[1:], halves[0]))
-    rest = [gains(ones[k], others[k], mix_share, norm_gain) for k in (1, 2)]
-    tops = factors_of(rest)
-    factors += [tops[0], tops[1]]
-    halves += [halves_of(rest[k - 1], factors[k]) for k in (1, 2)]
+    gained = [gains(one, other, mix_share, norm_gain) for one, other in zip(ones, others)]
+    tops = factors_of(gained)
+    factors = [tops[k] for k in range(3)]
+    halves = [halves_of(gained[k], factors[k]) for k in range(3)]
     plans = [gather_all(halves[k], n, me) for k in range(3)]
     finals = []
     for early, late in plans:
-        shape = (first.shape[0] * n, first.shape[1])
+        shape = (ones[0].shape[0] * n, ones[0].shape[1])
         out = place(*early, shape)
         if late[0]:
             out = place(*late, shape, out)

time: 247 us -> 238 us (0.964)
  blocking collectives: 19.9 us -> 10.7 us
    all_gather x2 -> x1, blocking collectives: 19.9 us -> 10.7 us  [factors_of(): return jnp.max(lax.all_gather(tops, 'rows', axis=0), axis=0)]
    reduce_max x2 -> x1, other arithmetic: 9.29 us -> 10.6 us  [factors_of(): tops = jnp.stack([jnp.max(jnp.abs(g), axis=0) for g in gained])]
  transfers between devices with their start and end apart: 42 -> 42, of which waited for: 18 -> 17; matrix products, arithmetic and copies ran while one was open for 1% -> 1% of each run, Pallas kernels for 13% -> 13%
where the time goes in v2:
time: 238 us; the launch traced here: 237 us
  waiting for transfers between devices  151 us (63%)
  Pallas kernels  35.5 us (15%)
  starting transfers between devices  22.6 us (9%)
  other arithmetic  15.4 us (6%)
  blocking collectives  10.7 us (4%)
    ppermute x42, waiting for transfers between devices, shift(): return lax.ppermute(x, 'rows', table)  151 us
    pallas_call x6, Pallas kernels, place(): pl.pallas_call(functools.partial(place_body, count, [p.shape[0] for p in...  35.5 us
    ppermute x42, starting transfers between devices, shift(): return lax.ppermute(x, 'rows', table)  22.6 us
    all_gather x1, blocking collectives, factors_of(): return jnp.max(lax.all_gather(tops, 'rows', axis=0), axis=0)  10.7 us
    reduce_max x1, other arithmetic, factors_of(): tops = jnp.stack([jnp.max(jnp.abs(g), axis=0) for g in gained])  10.6 us
  transfers between devices with their start and end apart: 42, of which 17 were waited for; matrix products, arithmetic and copies ran while one was open for 1% of the time, Pallas kernels for 13%

profile of v2, /device:TPU:0, one launch (start us, length us, event | category | flops | bytes accessed | tf_op | source)
XLA Modules:
  0.0 237.2 jit_solution(5885570466803102583)
XLA Ops:
  0.6 0.7 broadcast_subtract_fusion
  1.3 10.6 %abs_reduce_fusion.1 = (f32[1280]{0:T(1024)S(1)}, f32[640,1280]{1,0:T(8,128)}, f32[1280]{0:T(1024)S(1)}, f32[640,1280]{1,0:T(8,128)}, f32[1280]{0:T(1024)S(1)}, /*index=5*/f32[640,1280]{1,0:T(8,128)S(1)}) fusion(f32[640]{0:T(1024)} %param.15, f32[640,1280]{1,0:T(8,128)} %param.11, f32[640]{0:T(1024)S(1)} %broadcast_subtract_fusion, f32[640,1280]{1,0:T(8,128)} %param.10, ...), kind=kLoop, calls=%fused_computation.2 | loop fusion | flops 14741760 | bytes 29514240 | tf_op jit(solution)/shard_map/reduce_max | solution.py:108
  11.9 10.7 %all-gather.1 = f32[8,3,1280]{2,1,0:T(4,128)S(1)} all-gather(f32[1,3,1280]{2,1,0:T(4,128)S(1)} %maximum_bitcast_fusion), channel_id=2, replica_groups=mesh['rows'=8,'model'=4] {'rows'}, dimensions={0}, use_global_device_ids=true | all-gather | bytes 138240 | tf_op jit(solution)/shard_map/all_gather | solution.py:109
  22.8 2.3 fusion
  25.2 1.6 collective-permute-start.28
  26.7 0.5 collective-permute-start.30
  27.2 1.5 collective-permute-start.34
  28.7 0.5 collective-permute-start.35
  29.6 16.7 %collective-permute-done.28.refs_3_ = bf16[320,1280]{1,0:T(8,128)(2,1)S(1)} collective-permute-done((bf16[320,1280]{1,0:T(8,128)(2,1)S(1)}, bf16[320,1280]{1,0:T(8,128)(2,1)S(1)}, u32[]{:S(2)}, u32[]{:S(2)}) %collective-permute-start.28) | collective-permute-done | bytes 819232 | tf_op jit(solution)/shard_map/ppermute | solution.py:63
  46.3 1.5 collective-permute-done.30.refs_5_
  47.8 0.5 collective-permute-start.14
  48.4 15.5 %collective-permute-done.34.refs_4_ = bf16[320,1280]{1,0:T(8,128)(2,1)S(1)} collective-permute-done((bf16[320,1280]{1,0:T(8,128)(2,1)S(1)}, bf16[320,1280]{1,0:T(8,128)(2,1)S(1)}, u32[]{:S(2)}, u32[]{:S(2)}) %collective-permute-start.34) | collective-permute-done | bytes 819232 | tf_op jit(solution)/shard_map/ppermute | solution.py:63
  63.9 1.5 collective-permute-start.16
  65.4 0.5 collective-permute-start.20
  65.9 1.5 collective-permute-start.21
  67.4 14.0 %collective-permute-done.14.refs_3_ = bf16[320,1280]{1,0:T(8,128)(2,1)S(1)} collective-permute-done((bf16[320,1280]{1,0:T(8,128)(2,1)S(1)}, bf16[320,1280]{1,0:T(8,128)(2,1)S(1)}, u32[]{:S(2)}, u32[]{:S(2)}) %collective-permute-start.14) | collective-permute-done | bytes 819232 | tf_op jit(solution)/shard_map/ppermute | solution.py:63
  81.8 3.3 %collective-permute-done.16.refs_5_ = bf16[320,1280]{1,0:T(8,128)(2,1)S(1)} collective-permute-done((bf16[320,1280]{1,0:T(8,128)(2,1)S(1)}, bf16[320,1280]{1,0:T(8,128)(2,1)S(1)}, u32[]{:S(2)}, u32[]{:S(2)}) %collective-permute-start.16) | collective-permute-done | bytes 819232 | tf_op jit(solution)/shard_map/ppermute | solution.py:63
  85.0 1.5 collective-permute-start
  86.5 12.5 %collective-permute-done.20.refs_4_ = bf16[320,1280]{1,0:T(8,128)(2,1)S(1)} collective-permute-done((bf16[320,1280]{1,0:T(8,128)(2,1)S(1)}, bf16[320,1280]{1,0:T(8,128)(2,1)S(1)}, u32[]{:S(2)}, u32[]{:S(2)}) %collective-permute-start.20) | collective-permute-done | bytes 819232 | tf_op jit(solution)/shard_map/ppermute | solution.py:63
  99.0 1.5 collective-permute-start.2
  100.5 1.5 collective-permute-start.6
  102.0 0.6 collective-permute-start.7
  102.6 13.9 %collective-permute-done.refs_3_ = bf16[320,1280]{1,0:T(8,128)(2,1)S(1)} collective-permute-done((bf16[320,1280]{1,0:T(8,128)(2,1)S(1)}, bf16[320,1280]{1,0:T(8,128)(2,1)S(1)}, u32[]{:S(2)}, u32[]{:S(2)}) %collective-permute-start) | collective-permute-done | bytes 819232 | tf_op jit(solution)/shard_map/ppermute | solution.py:63
  116.6 3.5 %collective-permute-done.2.refs_5_ = bf16[320,1280]{1,0:T(8,128)(2,1)S(1)} collective-permute-done((bf16[320,1280]{1,0:T(8,128)(2,1)S(1)}, bf16[320,1280]{1,0:T(8,128)(2,1)S(1)}, u32[]{:S(2)}, u32[]{:S(2)}) %collective-permute-start.2) | collective-permute-done | bytes 819232 | tf_op jit(solution)/shard_map/ppermute | solution.py:63
  120.1 13.4 %collective-permute-done.6.refs_4_ = bf16[320,1280]{1,0:T(8,128)(2,1)S(1)} collective-permute-done((bf16[320,1280]{1,0:T(8,128)(2,1)S(1)}, bf16[320,1280]{1,0:T(8,128)(2,1)S(1)}, u32[]{:S(2)}, u32[]{:S(2)}) %collective-permute-start.6) | collective-permute-done | bytes 819232 | tf_op jit(solution)/shard_map/ppermute | solution.py:63
  133.5 2.1 collective-permute-done.7.refs_6_
  135.6 0.5 collective-permute-start.41
  136.1 1.5 collective-permute-start.29
  137.7 0.6 collective-permute-start.31
  139.2 17.2 %collective-permute-done.29.refs_1_ = bf16[320,1280]{1,0:T(8,128)(2,1)S(1)} collective-permute-done((bf16[320,1280]{1,0:T(8,128)(2,1)S(1)}, bf16[320,1280]{1,0:T(8,128)(2,1)S(1)}, u32[]{:S(2)}, u32[]{:S(2)}) %collective-permute-start.29) | collective-permute-done | bytes 819232 | tf_op jit(solution)/shard_map/ppermute | solution.py:63
  156.4 1.4 collective-permute-done.31.refs_2_
  157.8 0.5 collective-permute-start.15
  158.3 1.6 collective-permute-start.17
  160.6 16.6 %collective-permute-done.15.refs_1_ = bf16[320,1280]{1,0:T(8,128)(2,1)} collective-permute-done((bf16[320,1280]{1,0:T(8,128)(2,1)S(1)}, bf16[320,1280]{1,0:T(8,128)(2,1)}, u32[]{:S(2)}, u32[]{:S(2)}) %collective-permute-start.15) | collective-permute-done | bytes 819232 | tf_op jit(solution)/shard_map/ppermute | solution.py:63
  177.2 1.3 collective-permute-done.17.refs_2_
  178.5 0.5 collective-permute-start.1
  179.0 1.6 collective-permute-start.3
  181.3 16.7 %collective-permute-done.1.refs_1_ = bf16[320,1280]{1,0:T(8,128)(2,1)} collective-permute-done((bf16[320,1280]{1,0:T(8,128)(2,1)S(1)}, bf16[320,1280]{1,0:T(8,128)(2,1)}, u32[]{:S(2)}, u32[]{:S(2)}) %collective-permute-start.1) | collective-permute-done | bytes 819232 | tf_op jit(solution)/shard_map/ppermute | solution.py:63
  198.0 1.3 collective-permute-done.3.refs_2_
  199.4 0.6 collective-permute-start.5
  200.3 0.7 and_select_fusion.1.refs_0_
  201.0 0.6 and_select_fusion.refs_0_
  201.6 8.3 %shard_map.131.refs_5_ = bf16[5120,1280]{1,0:T(8,128)(2,1)} custom-call(s32[12]{0:T(128)} %and_select_fusion.refs_0_, bf16[320,1280]{1,0:T(8,128)(2,1)} %copy-done.2, bf16[320,1280]{1,0:T(8,128)(2,1)} %copy-done.1, bf16[320,1280]{1,0:T(8,128)(2,1)} %copy-done.7, bf16[320,1280]{1,0:T(8,128)(2,1)} %copy-done.9, bf16[320,1280]{1,0:T(8,128)(2,1)} %copy-done.8, ...), custom_call_target="tpu_custom_call" | custom-call | bytes 19660800 | tf_op jit(solution)/shard_map/pallas_call | solution.py:36
  209.9 8.3 %shard_map.129.refs_5_ = bf16[5120,1280]{1,0:T(8,128)(2,1)} custom-call(s32[12]{0:T(128)} %and_select_fusion.refs_0_, bf16[320,1280]{1,0:T(8,128)(2,1)} %copy-done.4, bf16[320,1280]{1,0:T(8,128)(2,1)} %copy-done.3, bf16[320,1280]{1,0:T(8,128)(2,1)} %copy-done.12, bf16[320,1280]{1,0:T(8,128)(2,1)} %copy-done.15, bf16[320,1280]{1,0:T(8,128)(2,1)} %copy-done.14, ...), custom_call_target="tpu_custom_call" | custom-call | bytes 19660800 | tf_op jit(solution)/shard_map/pallas_call | solution.py:36
  218.1 8.3 %shard_map.127.refs_5_ = bf16[5120,1280]{1,0:T(8,128)(2,1)} custom-call(s32[12]{0:T(128)} %and_select_fusion.refs_0_, bf16[320,1280]{1,0:T(8,128)(2,1)} %copy-done.6, bf16[320,1280]{1,0:T(8,128)(2,1)} %copy-done.5, bf16[320,1280]{1,0:T(8,128)(2,1)} %copy-done.19, bf16[320,1280]{1,0:T(8,128)(2,1)} %copy-done.21, bf16[320,1280]{1,0:T(8,128)(2,1)} %copy-done.20, ...), custom_call_target="tpu_custom_call" | custom-call | bytes 19660800 | tf_op jit(solution)/shard_map/pallas_call | solution.py:36
  226.4 3.6 %shard_map.132 = bf16[5120,1280]{1,0:T(8,128)(2,1)} custom-call(s32[4]{0:T(128)} %and_select_fusion.1.refs_0_, bf16[320,1280]{1,0:T(8,128)(2,1)} %copy-done.25, bf16[320,1280]{1,0:T(8,128)(2,1)} %collective-permute-done.31.refs_2_, bf16[320,1280]{1,0:T(8,128)(2,1)} %copy-done.38, ...), custom_call_target="tpu_custom_call", output_to_operand_aliasing={{}: (5, {})} | custom-call | bytes 6553600 | tf_op jit(solution)/shard_map/pallas_call | solution.py:36
  230.0 3.6 %shard_map.130 = bf16[5120,1280]{1,0:T(8,128)(2,1)} custom-call(s32[4]{0:T(128)} %and_select_fusion.1.refs_0_, bf16[320,1280]{1,0:T(8,128)(2,1)} %collective-permute-done.15.refs_1_, bf16[320,1280]{1,0:T(8,128)(2,1)} %collective-permute-done.17.refs_2_, bf16[320,1280]{1,0:T(8,128)(2,1)} %collective-permute-done.18.refs_3_, ...), custom_call_target="tpu_custom_call", output_to_operand_aliasing={{}: (5, {})} | custom-call | bytes 6553600 | tf_op jit(solution)/shard_map/pallas_call | solution.py:36
  233.6 3.6 %shard_map.128 = bf16[5120,1280]{1,0:T(8,128)(2,1)} custom-call(s32[4]{0:T(128)} %and_select_fusion.1.refs_0_, bf16[320,1280]{1,0:T(8,128)(2,1)} %collective-permute-done.1.refs_1_, bf16[320,1280]{1,0:T(8,128)(2,1)} %collective-permute-done.3.refs_2_, bf16[320,1280]{1,0:T(8,128)(2,1)} %collective-permute-done.4.refs_3_, ...), custom_call_target="tpu_custom_call", output_to_operand_aliasing={{}: (5, {})} | custom-call | bytes 6553600 | tf_op jit(solution)/shard_map/pallas_call | solution.py:36
  (141 shorter events, 3.5 us)
Async XLA Ops:
  25.2 21.2 %collective-permute-start.28 = (bf16[320,1280]{1,0:T(8,128)(2,1)S(1)}, bf16[320,1280]{1,0:T(8,128)(2,1)S(1)}, u32[]{:S(2)}, u32[]{:S(2)}) collective-permute-start(bf16[320,1280]{1,0:T(8,128)(2,1)S(1)} %get-tuple-element.16.refs_1_), channel_id=1, source_target_pairs={{0,8},{4,12},{8,0},{12,4},{16,24},{20,28},{24,16},{28,20},{1,9},{5... | collective-permute-start | bytes 2457608 | tf_op jit(solution)/shard_map/ppermute | solution.py:63
  26.7 21.1 %collective-permute-start.30 = (bf16[320,1280]{1,0:T(8,128)(2,1)S(1)}, bf16[320,1280]{1,0:T(8,128)(2,1)S(1)}, u32[]{:S(2)}, u32[]{:S(2)}) collective-permute-start(bf16[320,1280]{1,0:T(8,128)(2,1)S(1)} %get-tuple-element.15.refs_2_), channel_id=1, source_target_pairs={{0,16},{4,20},{8,24},{12,28},{16,0},{20,4},{24,8},{28,12},{1,17},{... | collective-permute-start | bytes 2457608 | tf_op jit(solution)/shard_map/ppermute | solution.py:63
  27.2 36.7 %collective-permute-start.34 = (bf16[320,1280]{1,0:T(8,128)(2,1)S(1)}, bf16[320,1280]{1,0:T(8,128)(2,1)S(1)}, u32[]{:S(2)}, u32[]{:S(2)}) collective-permute-start(bf16[320,1280]{1,0:T(8,128)(2,1)S(1)} %get-tuple-element.15.refs_2_), channel_id=1, source_target_pairs={{0,8},{4,12},{8,0},{12,4},{16,24},{20,28},{24,16},{28,20},{1,9},{5... | collective-permute-start | bytes 2457608 | tf_op jit(solution)/shard_map/ppermute | solution.py:63
  28.7 36.7 %collective-permute-start.35 = (bf16[320,1280]{1,0:T(8,128)(2,1)S(1)}, bf16[320,1280]{1,0:T(8,128)(2,1)S(1)}, u32[]{:S(2)}, u32[]{:S(2)}) collective-permute-start(bf16[320,1280]{1,0:T(8,128)(2,1)S(1)} %get-tuple-element.16.refs_1_), channel_id=1, source_target_pairs={{0,16},{4,20},{8,24},{12,28},{16,0},{20,4},{24,8},{28,12},{1,17},{... | collective-permute-start | bytes 2457608 | tf_op jit(solution)/shard_map/ppermute | solution.py:63
  29.3 36.7 %collective-permute-start.36 = (bf16[320,1280]{1,0:T(8,128)(2,1)S(1)}, bf16[320,1280]{1,0:T(8,128)(2,1)S(1)}, u32[]{:S(2)}, u32[]{:S(2)}) collective-permute-start(bf16[320,1280]{1,0:T(8,128)(2,1)S(1)} %get-tuple-element.16.refs_1_), channel_id=1, source_target_pairs={{0,4},{4,0},{8,12},{12,8},{16,20},{20,16},{24,28},{28,24},{1,5},{5... | collective-permute-start | bytes 2457608 | tf_op jit(solution)/shard_map/ppermute | solution.py:63
  46.3 21.1 %collective-permute-start.37 = (bf16[320,1280]{1,0:T(8,128)(2,1)S(1)}, bf16[320,1280]{1,0:T(8,128)(2,1)S(1)}, u32[]{:S(2)}, u32[]{:S(2)}) collective-permute-start(bf16[320,1280]{1,0:T(8,128)(2,1)S(1)} %get-tuple-element.15.refs_2_), channel_id=1, source_target_pairs={{0,4},{4,0},{8,12},{12,8},{16,20},{20,16},{24,28},{28,24},{1,5},{5... | collective-permute-start | bytes 2457608 | tf_op jit(solution)/shard_map/ppermute | solution.py:63
  47.8 108.6 %copy-start.8 = (bf16[320,1280]{1,0:T(8,128)(2,1)}, bf16[320,1280]{1,0:T(8,128)(2,1)S(1)}, u32[]{:S(2)}) copy-start(bf16[320,1280]{1,0:T(8,128)(2,1)S(1)} %collective-permute-done.30.refs_5_) | copy-start | bytes 2457604
  47.8 33.6 %collective-permute-start.14 = (bf16[320,1280]{1,0:T(8,128)(2,1)S(1)}, bf16[320,1280]{1,0:T(8,128)(2,1)S(1)}, u32[]{:S(2)}, u32[]{:S(2)}) collective-permute-start(bf16[320,1280]{1,0:T(8,128)(2,1)S(1)} %get-tuple-element.18.refs_1_), channel_id=1, source_target_pairs={{0,8},{4,12},{8,0},{12,4},{16,24},{20,28},{24,16},{28,20},{1,9},{5... | collective-permute-start | bytes 2457608 | tf_op jit(solution)/shard_map/ppermute | solution.py:63
  63.9 93.9 %copy-start.9 = (bf16[320,1280]{1,0:T(8,128)(2,1)}, bf16[320,1280]{1,0:T(8,128)(2,1)S(1)}, u32[]{:S(2)}) copy-start(bf16[320,1280]{1,0:T(8,128)(2,1)S(1)} %collective-permute-done.34.refs_4_) | copy-start | bytes 2457604
  63.9 21.1 %collective-permute-start.16 = (bf16[320,1280]{1,0:T(8,128)(2,1)S(1)}, bf16[320,1280]{1,0:T(8,128)(2,1)S(1)}, u32[]{:S(2)}, u32[]{:S(2)}) collective-permute-start(bf16[320,1280]{1,0:T(8,128)(2,1)S(1)} %get-tuple-element.17.refs_2_), channel_id=1, source_target_pairs={{0,16},{4,20},{8,24},{12,28},{16,0},{20,4},{24,8},{28,12},{1,17},{... | collective-permute-start | bytes 2457608 | tf_op jit(solution)/shard_map/ppermute | solution.py:63
  65.4 92.9 %copy-start.10 = (bf16[320,1280]{1,0:T(8,128)(2,1)}, bf16[320,1280]{1,0:T(8,128)(2,1)S(1)}, u32[]{:S(2)}) copy-start(bf16[320,1280]{1,0:T(8,128)(2,1)S(1)} %collective-permute-done.35.refs_6_) | copy-start | bytes 2457604
  65.4 33.6 %collective-permute-start.20 = (bf16[320,1280]{1,0:T(8,128)(2,1)S(1)}, bf16[320,1280]{1,0:T(8,128)(2,1)S(1)}, u32[]{:S(2)}, u32[]{:S(2)}) collective-permute-start(bf16[320,1280]{1,0:T(8,128)(2,1)S(1)} %get-tuple-element.17.refs_2_), channel_id=1, source_target_pairs={{0,8},{4,12},{8,0},{12,4},{16,24},{20,28},{24,16},{28,20},{1,9},{5... | collective-permute-start | bytes 2457608 | tf_op jit(solution)/shard_map/ppermute | solution.py:63
  65.9 92.4 %copy-start.11 = (bf16[320,1280]{1,0:T(8,128)(2,1)}, bf16[320,1280]{1,0:T(8,128)(2,1)S(1)}, u32[]{:S(2)}) copy-start(bf16[320,1280]{1,0:T(8,128)(2,1)S(1)} %collective-permute-done.36.refs_7_) | copy-start | bytes 2457604
  65.9 34.6 %collective-permute-start.21 = (bf16[320,1280]{1,0:T(8,128)(2,1)S(1)}, bf16[320,1280]{1,0:T(8,128)(2,1)S(1)}, u32[]{:S(2)}, u32[]{:S(2)}) collective-permute-start(bf16[320,1280]{1,0:T(8,128)(2,1)S(1)} %get-tuple-element.18.refs_1_), channel_id=1, source_target_pairs={{0,16},{4,20},{8,24},{12,28},{16,0},{20,4},{24,8},{28,12},{1,17},{... | collective-permute-start | bytes 2457608 | tf_op jit(solution)/shard_map/ppermute | solution.py:63
  67.4 109.7 %copy-start.13 = (bf16[320,1280]{1,0:T(8,128)(2,1)}, bf16[320,1280]{1,0:T(8,128)(2,1)S(1)}, u32[]{:S(2)}) copy-start(bf16[320,1280]{1,0:T(8,128)(2,1)S(1)} %collective-permute-done.37.refs_8_) | copy-start | bytes 2457604
  67.4 34.5 %collective-permute-start.22 = (bf16[320,1280]{1,0:T(8,128)(2,1)S(1)}, bf16[320,1280]{1,0:T(8,128)(2,1)S(1)}, u32[]{:S(2)}, u32[]{:S(2)}) collective-permute-start(bf16[320,1280]{1,0:T(8,128)(2,1)S(1)} %get-tuple-element.18.refs_1_), channel_id=1, source_target_pairs={{0,4},{4,0},{8,12},{12,8},{16,20},{20,16},{24,28},{28,24},{1,5},{5... | collective-permute-start | bytes 2457608 | tf_op jit(solution)/shard_map/ppermute | solution.py:63
  81.5 21.1 %collective-permute-start.23 = (bf16[320,1280]{1,0:T(8,128)(2,1)S(1)}, bf16[320,1280]{1,0:T(8,128)(2,1)S(1)}, u32[]{:S(2)}, u32[]{:S(2)}) collective-permute-start(bf16[320,1280]{1,0:T(8,128)(2,1)S(1)} %get-tuple-element.17.refs_2_), channel_id=1, source_target_pairs={{0,4},{4,0},{8,12},{12,8},{16,20},{20,16},{24,28},{28,24},{1,5},{5... | collective-permute-start | bytes 2457608 | tf_op jit(solution)/shard_map/ppermute | solution.py:63
  85.0 31.5 %collective-permute-start = (bf16[320,1280]{1,0:T(8,128)(2,1)S(1)}, bf16[320,1280]{1,0:T(8,128)(2,1)S(1)}, u32[]{:S(2)}, u32[]{:S(2)}) collective-permute-start(bf16[320,1280]{1,0:T(8,128)(2,1)S(1)} %get-tuple-element.20.refs_1_), channel_id=1, source_target_pairs={{0,8},{4,12},{8,0},{12,4},{16,24},{20,28},{24,16},{28,20},{1,9},{5... | collective-permute-start | bytes 2457608 | tf_op jit(solution)/shard_map/ppermute | solution.py:63
  99.0 21.1 %collective-permute-start.2 = (bf16[320,1280]{1,0:T(8,128)(2,1)S(1)}, bf16[320,1280]{1,0:T(8,128)(2,1)S(1)}, u32[]{:S(2)}, u32[]{:S(2)}) collective-permute-start(bf16[320,1280]{1,0:T(8,128)(2,1)S(1)} %get-tuple-element.19.refs_2_), channel_id=1, source_target_pairs={{0,16},{4,20},{8,24},{12,28},{16,0},{20,4},{24,8},{28,12},{1,17},{... | collective-permute-start | bytes 2457608 | tf_op jit(solution)/shard_map/ppermute | solution.py:63
  100.5 33.0 %collective-permute-start.6 = (bf16[320,1280]{1,0:T(8,128)(2,1)S(1)}, bf16[320,1280]{1,0:T(8,128)(2,1)S(1)}, u32[]{:S(2)}, u32[]{:S(2)}) collective-permute-start(bf16[320,1280]{1,0:T(8,128)(2,1)S(1)} %get-tuple-element.19.refs_2_), channel_id=1, source_target_pairs={{0,8},{4,12},{8,0},{12,4},{16,24},{20,28},{24,16},{28,20},{1,9},{5... | collective-permute-start | bytes 2457608 | tf_op jit(solution)/shard_map/ppermute | solution.py:63
  102.0 33.6 %collective-permute-start.7 = (bf16[320,1280]{1,0:T(8,128)(2,1)S(1)}, bf16[320,1280]{1,0:T(8,128)(2,1)S(1)}, u32[]{:S(2)}, u32[]{:S(2)}) collective-permute-start(bf16[320,1280]{1,0:T(8,128)(2,1)S(1)} %get-tuple-element.20.refs_1_), channel_id=1, source_target_pairs={{0,16},{4,20},{8,24},{12,28},{16,0},{20,4},{24,8},{28,12},{1,17},{... | collective-permute-start | bytes 2457608 | tf_op jit(solution)/shard_map/ppermute | solution.py:63
  102.5 33.0 %collective-permute-start.8 = (bf16[320,1280]{1,0:T(8,128)(2,1)S(1)}, bf16[320,1280]{1,0:T(8,128)(2,1)S(1)}, u32[]{:S(2)}, u32[]{:S(2)}) collective-permute-start(bf16[320,1280]{1,0:T(8,128)(2,1)S(1)} %get-tuple-element.20.refs_1_), channel_id=1, source_target_pairs={{0,4},{4,0},{8,12},{12,8},{16,20},{20,16},{24,28},{28,24},{1,5},{5... | collective-permute-start | bytes 2457608 | tf_op jit(solution)/shard_map/ppermute | solution.py:63
  116.6 93.3 %copy-start.19 = (bf16[320,1280]{1,0:T(8,128)(2,1)}, bf16[320,1280]{1,0:T(8,128)(2,1)S(1)}, u32[]{:S(2)}) copy-start(bf16[320,1280]{1,0:T(8,128)(2,1)S(1)} %collective-permute-done.refs_3_) | copy-start | bytes 2457604
  116.6 19.5 %collective-permute-start.9 = (bf16[320,1280]{1,0:T(8,128)(2,1)S(1)}, bf16[320,1280]{1,0:T(8,128)(2,1)S(1)}, u32[]{:S(2)}, u32[]{:S(2)}) collective-permute-start(bf16[320,1280]{1,0:T(8,128)(2,1)S(1)} %get-tuple-element.19.refs_2_), channel_id=1, source_target_pairs={{0,4},{4,0},{8,12},{12,8},{16,20},{20,16},{24,28},{28,24},{1,5},{5... | collective-permute-start | bytes 2457608 | tf_op jit(solution)/shard_map/ppermute | solution.py:63
  120.1 17.5 %collective-permute-start.38 = (bf16[320,1280]{1,0:T(8,128)(2,1)S(1)}, bf16[320,1280]{1,0:T(8,128)(2,1)S(1)}, u32[]{:S(2)}, u32[]{:S(2)}) collective-permute-start(bf16[320,1280]{1,0:T(8,128)(2,1)S(1)} %collective-permute-done.28.refs_3_), channel_id=1, source_target_pairs={{0,4},{4,0},{8,12},{12,8},{16,20},{20,16},{24,28},{28,24},{1,5},{5... | collective-permute-start | bytes 2457608 | tf_op jit(solution)/shard_map/ppermute | solution.py:63
  133.5 4.8 %collective-permute-start.40 = (bf16[320,1280]{1,0:T(8,128)(2,1)S(1)}, bf16[320,1280]{1,0:T(8,128)(2,1)S(1)}, u32[]{:S(2)}, u32[]{:S(2)}) collective-permute-start(bf16[320,1280]{1,0:T(8,128)(2,1)S(1)} %collective-permute-done.30.refs_5_), channel_id=1, source_target_pairs={{0,4},{4,0},{8,12},{12,8},{16,20},{20,16},{24,28},{28,24},{1,5},{5... | collective-permute-start | bytes 2457608 | tf_op jit(solution)/shard_map/ppermute | solution.py:63
  135.6 2.7 %collective-permute-start.39 = (bf16[320,1280]{1,0:T(8,128)(2,1)S(1)}, bf16[320,1280]{1,0:T(8,128)(2,1)S(1)}, u32[]{:S(2)}, u32[]{:S(2)}) collective-permute-start(bf16[320,1280]{1,0:T(8,128)(2,1)S(1)} %collective-permute-done.34.refs_4_), channel_id=1, source_target_pairs={{0,4},{4,0},{8,12},{12,8},{16,20},{20,16},{24,28},{28,24},{1,5},{5... | collective-permute-start | bytes 2457608 | tf_op jit(solution)/shard_map/ppermute | solution.py:63
  135.6 3.5 %collective-permute-start.41 = (bf16[320,1280]{1,0:T(8,128)(2,1)S(1)}, bf16[320,1280]{1,0:T(8,128)(2,1)S(1)}, u32[]{:S(2)}, u32[]{:S(2)}) collective-permute-start(bf16[320,1280]{1,0:T(8,128)(2,1)S(1)} %collective-permute-done.35.refs_6_), channel_id=1, source_target_pairs={{0,4},{4,0},{8,12},{12,8},{16,20},{20,16},{24,28},{28,24},{1,5},{5... | collective-permute-start | bytes 2457608 | tf_op jit(solution)/shard_map/ppermute | solution.py:63
  136.1 20.3 %collective-permute-start.29 = (bf16[320,1280]{1,0:T(8,128)(2,1)S(1)}, bf16[320,1280]{1,0:T(8,128)(2,1)S(1)}, u32[]{:S(2)}, u32[]{:S(2)}) collective-permute-start(bf16[320,1280]{1,0:T(8,128)(2,1)S(1)} %collective-permute-done.28.refs_3_), channel_id=1, source_target_pairs={{0,16},{4,20},{8,24},{12,28},{16,0},{20,4},{24,8},{28,12},{1,17},{... | collective-permute-start | bytes 2457608 | tf_op jit(solution)/shard_map/ppermute | solution.py:63
  137.7 20.1 %collective-permute-start.31 = (bf16[320,1280]{1,0:T(8,128)(2,1)S(1)}, bf16[320,1280]{1,0:T(8,128)(2,1)}, u32[]{:S(2)}, u32[]{:S(2)}) collective-permute-start(bf16[320,1280]{1,0:T(8,128)(2,1)S(1)} %collective-permute-done.30.refs_5_), channel_id=1, source_target_pairs={{0,8},{4,12},{8,0},{12,4},{16,24},{20,28},{24,16},{28,20},{1,9},{5... | collective-permute-start | bytes 2457608 | tf_op jit(solution)/shard_map/ppermute | solution.py:63
  138.3 20.1 %collective-permute-start.24 = (bf16[320,1280]{1,0:T(8,128)(2,1)S(1)}, bf16[320,1280]{1,0:T(8,128)(2,1)S(1)}, u32[]{:S(2)}, u32[]{:S(2)}) collective-permute-start(bf16[320,1280]{1,0:T(8,128)(2,1)S(1)} %collective-permute-done.14.refs_3_), channel_id=1, source_target_pairs={{0,4},{4,0},{8,12},{12,8},{16,20},{20,16},{24,28},{28,24},{1,5},{5... | collective-permute-start | bytes 2457608 | tf_op jit(solution)/shard_map/ppermute | solution.py:63
  138.3 21.6 %collective-permute-start.26 = (bf16[320,1280]{1,0:T(8,128)(2,1)S(1)}, bf16[320,1280]{1,0:T(8,128)(2,1)S(1)}, u32[]{:S(2)}, u32[]{:S(2)}) collective-permute-start(bf16[320,1280]{1,0:T(8,128)(2,1)S(1)} %collective-permute-done.16.refs_5_), channel_id=1, source_target_pairs={{0,4},{4,0},{8,12},{12,8},{16,20},{20,16},{24,28},{28,24},{1,5},{5... | collective-permute-start | bytes 2457608 | tf_op jit(solution)/shard_map/ppermute | solution.py:63
  139.1 20.9 %collective-permute-start.25 = (bf16[320,1280]{1,0:T(8,128)(2,1)S(1)}, bf16[320,1280]{1,0:T(8,128)(2,1)S(1)}, u32[]{:S(2)}, u32[]{:S(2)}) collective-permute-start(bf16[320,1280]{1,0:T(8,128)(2,1)S(1)} %collective-permute-done.20.refs_4_), channel_id=1, source_target_pairs={{0,4},{4,0},{8,12},{12,8},{16,20},{20,16},{24,28},{28,24},{1,5},{5... | collective-permute-start | bytes 2457608 | tf_op jit(solution)/shard_map/ppermute | solution.py:63
  156.4 4.1 %collective-permute-start.27 = (bf16[320,1280]{1,0:T(8,128)(2,1)S(1)}, bf16[320,1280]{1,0:T(8,128)(2,1)S(1)}, u32[]{:S(2)}, u32[]{:S(2)}) collective-permute-start(bf16[320,1280]{1,0:T(8,128)(2,1)S(1)} %collective-permute-done.21.refs_6_), channel_id=1, source_target_pairs={{0,4},{4,0},{8,12},{12,8},{16,20},{20,16},{24,28},{28,24},{1,5},{5... | collective-permute-start | bytes 2457608 | tf_op jit(solution)/shard_map/ppermute | solution.py:63
  157.8 19.4 %collective-permute-start.15 = (bf16[320,1280]{1,0:T(8,128)(2,1)S(1)}, bf16[320,1280]{1,0:T(8,128)(2,1)}, u32[]{:S(2)}, u32[]{:S(2)}) collective-permute-start(bf16[320,1280]{1,0:T(8,128)(2,1)S(1)} %collective-permute-done.14.refs_3_), channel_id=1, source_target_pairs={{0,16},{4,20},{8,24},{12,28},{16,0},{20,4},{24,8},{28,12},{1,17},{... | collective-permute-start | bytes 2457608 | tf_op jit(solution)/shard_map/ppermute | solution.py:63
  158.3 20.1 %collective-permute-start.17 = (bf16[320,1280]{1,0:T(8,128)(2,1)S(1)}, bf16[320,1280]{1,0:T(8,128)(2,1)}, u32[]{:S(2)}, u32[]{:S(2)}) collective-permute-start(bf16[320,1280]{1,0:T(8,128)(2,1)S(1)} %collective-permute-done.16.refs_5_), channel_id=1, source_target_pairs={{0,8},{4,12},{8,0},{12,4},{16,24},{20,28},{24,16},{28,20},{1,9},{5... | collective-permute-start | bytes 2457608 | tf_op jit(solution)/shard_map/ppermute | solution.py:63
  159.9 19.1 %collective-permute-start.10 = (bf16[320,1280]{1,0:T(8,128)(2,1)S(1)}, bf16[320,1280]{1,0:T(8,128)(2,1)S(1)}, u32[]{:S(2)}, u32[]{:S(2)}) collective-permute-start(bf16[320,1280]{1,0:T(8,128)(2,1)S(1)} %collective-permute-done.refs_3_), channel_id=1, source_target_pairs={{0,4},{4,0},{8,12},{12,8},{16,20},{20,16},{24,28},{28,24},{1,5},{5... | collective-permute-start | bytes 2457608 | tf_op jit(solution)/shard_map/ppermute | solution.py:63
  160.0 20.6 %collective-permute-start.12 = (bf16[320,1280]{1,0:T(8,128)(2,1)S(1)}, bf16[320,1280]{1,0:T(8,128)(2,1)S(1)}, u32[]{:S(2)}, u32[]{:S(2)}) collective-permute-start(bf16[320,1280]{1,0:T(8,128)(2,1)S(1)} %collective-permute-done.2.refs_5_), channel_id=1, source_target_pairs={{0,4},{4,0},{8,12},{12,8},{16,20},{20,16},{24,28},{28,24},{1,5},{5... | collective-permute-start | bytes 2457608 | tf_op jit(solution)/shard_map/ppermute | solution.py:63
  160.5 20.2 %collective-permute-start.11 = (bf16[320,1280]{1,0:T(8,128)(2,1)S(1)}, bf16[320,1280]{1,0:T(8,128)(2,1)S(1)}, u32[]{:S(2)}, u32[]{:S(2)}) collective-permute-start(bf16[320,1280]{1,0:T(8,128)(2,1)S(1)} %collective-permute-done.6.refs_4_), channel_id=1, source_target_pairs={{0,4},{4,0},{8,12},{12,8},{16,20},{20,16},{24,28},{28,24},{1,5},{5... | collective-permute-start | bytes 2457608 | tf_op jit(solution)/shard_map/ppermute | solution.py:63
  177.2 4.0 %collective-permute-start.13 = (bf16[320,1280]{1,0:T(8,128)(2,1)S(1)}, bf16[320,1280]{1,0:T(8,128)(2,1)S(1)}, u32[]{:S(2)}, u32[]{:S(2)}) collective-permute-start(bf16[320,1280]{1,0:T(8,128)(2,1)S(1)} %collective-permute-done.7.refs_6_), channel_id=1, source_target_pairs={{0,4},{4,0},{8,12},{12,8},{16,20},{20,16},{24,28},{28,24},{1,5},{5... | collective-permute-start | bytes 2457608 | tf_op jit(solution)/shard_map/ppermute | solution.py:63
  178.5 19.5 %collective-permute-start.1 = (bf16[320,1280]{1,0:T(8,128)(2,1)S(1)}, bf16[320,1280]{1,0:T(8,128)(2,1)}, u32[]{:S(2)}, u32[]{:S(2)}) collective-permute-start(bf16[320,1280]{1,0:T(8,128)(2,1)S(1)} %collective-permute-done.refs_3_), channel_id=1, source_target_pairs={{0,16},{4,20},{8,24},{12,28},{16,0},{20,4},{24,8},{28,12},{1,17},{... | collective-permute-start | bytes 2457608 | tf_op jit(solution)/shard_map/ppermute | solution.py:63
  179.0 20.3 %collective-permute-start.3 = (bf16[320,1280]{1,0:T(8,128)(2,1)S(1)}, bf16[320,1280]{1,0:T(8,128)(2,1)}, u32[]{:S(2)}, u32[]{:S(2)}) collective-permute-start(bf16[320,1280]{1,0:T(8,128)(2,1)S(1)} %collective-permute-done.2.refs_5_), channel_id=1, source_target_pairs={{0,8},{4,12},{8,0},{12,4},{16,24},{20,28},{24,16},{28,20},{1,9},{5... | collective-permute-start | bytes 2457608 | tf_op jit(solution)/shard_map/ppermute | solution.py:63
  180.6 18.7 %collective-permute-start.32 = (bf16[320,1280]{1,0:T(8,128)(2,1)S(1)}, bf16[320,1280]{1,0:T(8,128)(2,1)S(1)}, u32[]{:S(2)}, u32[]{:S(2)}) collective-permute-start(bf16[320,1280]{1,0:T(8,128)(2,1)S(1)} %collective-permute-done.29.refs_1_), channel_id=1, source_target_pairs={{0,4},{4,0},{8,12},{12,8},{16,20},{20,16},{24,28},{28,24},{1,5},{5... | collective-permute-start | bytes 2457608 | tf_op jit(solution)/shard_map/ppermute | solution.py:63
  180.7 45.7 %collective-permute-start.33 = (bf16[320,1280]{1,0:T(8,128)(2,1)}, bf16[320,1280]{1,0:T(8,128)(2,1)}, u32[]{:S(2)}, u32[]{:S(2)}) collective-permute-start(bf16[320,1280]{1,0:T(8,128)(2,1)} %collective-permute-done.31.refs_2_), channel_id=1, source_target_pairs={{0,4},{4,0},{8,12},{12,8},{16,20},{20,16},{24,28},{28,24},{1,5},{5... | collective-permute-start | bytes 2457608 | tf_op jit(solution)/shard_map/ppermute | solution.py:63
  181.2 48.8 %collective-permute-start.18 = (bf16[320,1280]{1,0:T(8,128)(2,1)}, bf16[320,1280]{1,0:T(8,128)(2,1)}, u32[]{:S(2)}, u32[]{:S(2)}) collective-permute-start(bf16[320,1280]{1,0:T(8,128)(2,1)} %collective-permute-done.15.refs_1_), channel_id=1, source_target_pairs={{0,4},{4,0},{8,12},{12,8},{16,20},{20,16},{24,28},{28,24},{1,5},{5... | collective-permute-start | bytes 2457608 | tf_op jit(solution)/shard_map/ppermute | solution.py:63
  198.0 32.0 %collective-permute-start.19 = (bf16[320,1280]{1,0:T(8,128)(2,1)}, bf16[320,1280]{1,0:T(8,128)(2,1)}, u32[]{:S(2)}, u32[]{:S(2)}) collective-permute-start(bf16[320,1280]{1,0:T(8,128)(2,1)} %collective-permute-done.17.refs_2_), channel_id=1, source_target_pairs={{0,4},{4,0},{8,12},{12,8},{16,20},{20,16},{24,28},{28,24},{1,5},{5... | collective-permute-start | bytes 2457608 | tf_op jit(solution)/shard_map/ppermute | solution.py:63
  199.3 34.3 %collective-permute-start.4 = (bf16[320,1280]{1,0:T(8,128)(2,1)}, bf16[320,1280]{1,0:T(8,128)(2,1)}, u32[]{:S(2)}, u32[]{:S(2)}) collective-permute-start(bf16[320,1280]{1,0:T(8,128)(2,1)} %collective-permute-done.1.refs_1_), channel_id=1, source_target_pairs={{0,4},{4,0},{8,12},{12,8},{16,20},{20,16},{24,28},{28,24},{1,5},{5... | collective-permute-start | bytes 2457608 | tf_op jit(solution)/shard_map/ppermute | solution.py:63
  199.4 34.3 %collective-permute-start.5 = (bf16[320,1280]{1,0:T(8,128)(2,1)}, bf16[320,1280]{1,0:T(8,128)(2,1)}, u32[]{:S(2)}, u32[]{:S(2)}) collective-permute-start(bf16[320,1280]{1,0:T(8,128)(2,1)} %collective-permute-done.3.refs_2_), channel_id=1, source_target_pairs={{0,4},{4,0},{8,12},{12,8},{16,20},{20,16},{24,28},{28,24},{1,5},{5... | collective-permute-start | bytes 2457608 | tf_op jit(solution)/shard_map/ppermute | solution.py:63
  (36 other events, 1881.6 us)
